TPU v7x, 32 devices: a whole 2x2x4 slice. The times are simulated.
32 devices in a mesh: dp: 8 (over y, x, core), tensor: 4 (over z).
Axes of the slice: x: 2, y: 2, z: 4, core: 2. Of those that a mesh axis runs over, the one named last changes fastest.
Arguments:
- momentum: float32 [8, 5120, 1024], P('dp', None, 'tensor'), may hold values from -6 to 6
- activations: bfloat16 [4096, 5120], P(('dp', 'tensor')), may hold values from -6 to 6
- out_grads: bfloat16 [4096, 1024], P('dp', 'tensor'), may hold values from -0.29882812 to 0.29882812
- positions: int32 [8, 16, 4, 5120], P('dp', 'tensor'), may hold values from 0 to 63, as said below
Outputs:
- new_momentum: float32 [8, 5120, 1024], P('dp', None, 'tensor')
- update: bfloat16 [5120, 1024], P(None, 'tensor')
Inputs may be any that keep to these rules, and one draw needn't show every extreme that they name: The 4 positions of one block of one row of one replica are all different.
All inputs are finite; a program needn't handle non-finite values.
Results may differ from a plain program's by a relative error of at most 0.00075.
Values may be sent and summed in bfloat16 or wider, within the bound.
No kernel may reach another device: no remote copies, remote signals or barrier semaphores. Data moves between devices by JAX's collectives and lax.ppermute only.
A program may use at most 128 MiB of HBM per device.

v0:
```python
import functools

import jax
import jax.numpy as jnp
import numpy as np
from jax import lax
from jax.experimental import pallas as pl
from jax.experimental.pallas import tpu as pltpu
from jax.sharding import PartitionSpec as P


SPAN = 64
SUB = 256
LANES = 128
CODE_TOP = 32764.0
LN2 = 0.6931471805599453
VMEM_LIMIT = 40 * 1024 * 1024
CHUNKS = (6, 6, 4, 4)
GROUPS = ((0, 1), (2, 3))


def basis_parts(spans):
    freq = np.arange(SPAN, dtype=np.float64)[:, None]
    place = np.arange(SPAN, dtype=np.float64)[None, :]
    scales = np.where(freq == 0, (1.0 / SPAN) ** 0.5, (2.0 / SPAN) ** 0.5)
    table = scales * np.cos(np.pi * (2.0 * place + 1.0) * freq / (2 * SPAN))
    whole = np.kron(np.eye(spans), table).astype(np.float32)
    high = whole.astype(jnp.bfloat16)
    low = (whole - high.astype(np.float32)).astype(jnp.bfloat16)
    return np.stack([high, low, high.T, low.T])


def dot32(a, b):
    return lax.dot_general(a, b, (((1,), (0,)), ((), ())), preferred_element_type=jnp.float32)


def dot_split(high, low, x):
    x_high = x.astype(jnp.bfloat16)
    x_low = (x - x_high.astype(jnp.float32)).astype(jnp.bfloat16)
    return dot32(high, x_high) + (dot32(high, x_low) + dot32(low, x_high))


def lanes_at(i, offset=0):
    return pl.ds(pl.multiple_of(offset + i * SUB, SUB), SUB)


def line_blocks(grads_ref, tokens, roles):
    index = lax.axis_index("tensor")
    middle = (index == 1) | (index == 2)
    sources = (index, 3 * (index - 1), 3 - index, 6 - 3 * index)
    parts = []
    for k in roles:
        at = pl.multiple_of(jnp.clip(sources[k], 0, 3) * tokens, tokens)
        part = grads_ref[pl.ds(at, tokens)].T
        parts.append(part if k == 0 else jnp.where(middle, part, jnp.zeros_like(part)))
    return jnp.concatenate(parts, axis=1)


def pairs_of(count, work):
    if count % 2 == 0:
        lax.fori_loop(0, count // 2, lambda i, c: work((2 * i, 2 * i + 1)), None)
    else:
        lax.fori_loop(0, count, lambda i, c: work((i,)), None)


def partial_kernel(count, start, grads_ref, *refs):
    act_refs, out_ref = refs[:3], refs[3]
    act_buf, out_buf, blocks_ref, in_sem, out_sem = refs[4:]
    cols, tokens = grads_ref.shape[1], act_refs[0].shape[0]

    def copy_in(k, i):
        offset = start if k == 0 else 0
        return pltpu.make_async_copy(
            act_refs[k].at[:, lanes_at(i, offset)],
            act_buf.at[pl.ds(k * tokens, tokens), lanes_at(i)],
            in_sem.at[k, i],
        )

    def copy_out(i):
        return pltpu.make_async_copy(
            out_buf.at[:, lanes_at(i)], out_ref.at[:, lanes_at(i)], out_sem.at[i]
        )

    for i in range(count):
        for k in range(len(act_refs)):
            copy_in(k, i).start()

    blocks_ref[...] = line_blocks(grads_ref, tokens, (0, 2, 3))

    def one(i):
        for k in range(len(act_refs)):
            copy_in(k, i).wait()
        part = dot32(blocks_ref[...], act_buf[:, lanes_at(i)])
        top = jnp.maximum(jnp.max(jnp.abs(part), axis=0, keepdims=True), 1e-30)
        level = jnp.floor(jnp.log(top) * (1.0 / LN2)) + 1.0
        code = jnp.round(part * (CODE_TOP * jnp.exp(-level * LN2)))
        out_buf[:cols, lanes_at(i)] = code.astype(jnp.int32).astype(jnp.int16)
        extra = jnp.broadcast_to(level.astype(jnp.int32), (out_buf.shape[0] - cols, SUB))
        out_buf[cols:, lanes_at(i)] = extra.astype(jnp.int16)
        copy_out(i).start()

    def work(tiles):
        for i in tiles:
            one(i)

    pairs_of(count, work)
    for i in range(count):
        copy_out(i).wait()


def grad_kernel(n_act, has_part, slots, count, start, base, *refs):
    basis_ref, grads_ref, moment_ref, picks_ref = refs[:4]
    act_refs = refs[4 : 4 + n_act]
    part_ref = refs[4 + n_act] if has_part else None
    new_ref, record_ref = refs[-15:-13]
    moment_buf, picks_buf, act_buf, part_buf, new_buf, record_buf = refs[-13:-7]
    coeffs_refs, tile_refs, blocks_ref, in_sem, out_sem = refs[-7:-5], refs[-5:-3], *refs[-3:]
    cols = moment_ref.shape[2]
    spans = cols // SPAN
    tokens = act_refs[0].shape[0]
    ids = lax.broadcasted_iota(jnp.int32, (SPAN, LANES), 0)

    def copies_in(i):
        pairs = [
            (moment_ref.at[0, lanes_at(i, start)], moment_buf.at[i]),
            (picks_ref.at[0, :, :, lanes_at(i, start)], picks_buf.at[i]),
        ]
        for k, ref in enumerate(act_refs):
            offset = start if k == 0 else 0
            pairs.append(
                (ref.at[:, lanes_at(i, offset)], act_buf.at[i, pl.ds(k * tokens, tokens)])
            )
        if has_part:
            pairs.append((part_ref.at[:, lanes_at(i)], part_buf.at[i]))
        return [pltpu.make_async_copy(a, b, in_sem.at[k, i]) for k, (a, b) in enumerate(pairs)]

    def copies_out(i):
        return [
            pltpu.make_async_copy(
                new_buf.at[i], new_ref.at[0, lanes_at(i, start)], out_sem.at[0, i]
            ),
            pltpu.make_async_copy(
                record_buf.at[i], record_ref.at[:, lanes_at(i, start - base)], out_sem.at[1, i]
            ),
        ]

    for i in range(count):
        for copy in copies_in(i):
            copy.start()

    if n_act > 1:
        blocks_ref[...] = line_blocks(grads_ref, tokens, (0, 1, 2, 3))
    else:
        blocks_ref[...] = grads_ref[...].T

    def gather(i, coeffs_ref):
        for copy in copies_in(i):
            copy.wait()
        total = 0.9 * moment_buf[i].T + dot32(blocks_ref[...], act_buf[i])
        if has_part:
            level = part_buf[i, cols:][:1].astype(jnp.int32).astype(jnp.float32)
            code = part_buf[i, :cols].astype(jnp.int32).astype(jnp.float32)
            total = total + code * (jnp.exp(level * LN2) * (1.0 / CODE_TOP))
        coeffs_ref[...] = dot_split(basis_ref[0], basis_ref[1], total)
        return total

    def pick(i, coeffs_ref, tile_ref):
        for lo in range(0, SUB, LANES):
            lanes = slice(lo, lo + LANES)
            for b in range(spans):
                block = coeffs_ref[b * SPAN : (b + 1) * SPAN, lanes]
                tile = jnp.zeros_like(block)
                code = jnp.zeros((1, LANES), jnp.int32)
                for j in range(slots):
                    place = picks_buf[i, b, j : j + 1, lanes]
                    hit = place == ids
                    value = jnp.sum(jnp.where(hit, block, 0.0), axis=0, keepdims=True)
                    tile = jnp.where(hit, block, tile)
                    record_buf[i, b * slots + j : b * slots + j + 1, lanes] = value
                    code = code + place * SPAN**j
                tile_ref[b * SPAN : (b + 1) * SPAN, lanes] = tile
                row = spans * slots + b
                record_buf[i, row : row + 1, lanes] = code.astype(jnp.float32)

    def finish(i, total, tile_ref):
        restored = dot_split(basis_ref[2], basis_ref[3], tile_ref[...])
        new_buf[i] = (total - restored).T
        for copy in copies_out(i):
            copy.start()

    def work(tiles):
        totals = [gather(i, coeffs_refs[k]) for k, i in enumerate(tiles)]
        for k, i in enumerate(tiles):
            pick(i, coeffs_refs[k], tile_refs[k])
            finish(i, totals[k], tile_refs[k])

    pairs_of(count, work)
    for i in range(count):
        for copy in copies_out(i):
            copy.wait()


def sum_kernel(n_rec, slots, count, *refs):
    basis_ref = refs[0]
    record_refs = refs[1 : 1 + n_rec]
    decoded_ref, squares_ref, record_buf, decoded_buf = refs[1 + n_rec : 5 + n_rec]
    place_ref, tile_refs, in_sem, out_sem = refs[5 + n_rec], refs[6 + n_rec : 8 + n_rec], *refs[8 + n_rec :]
    cols = decoded_ref.shape[0]
    spans = cols // SPAN
    ids = lax.broadcasted_iota(jnp.int32, (SPAN, LANES), 0)

    def copy_in(k, i):
        return pltpu.make_async_copy(
            record_refs[k].at[:, lanes_at(i)], record_buf.at[k, i], in_sem.at[k, i]
        )

    def copy_out(i):
        return pltpu.make_async_copy(
            decoded_buf.at[i], decoded_ref.at[:, lanes_at(i)], out_sem.at[i]
        )

    for i in range(count):
        for k in range(n_rec):
            copy_in(k, i).start()

    def spread(slot, i):
        for k in range(n_rec):
            copy_in(k, i).wait()
            code = record_buf[k, i, spans * slots :].astype(jnp.int32)
            for j in range(slots):
                place_ref[slot, k, j] = lax.shift_right_logical(code, 6 * j) & (SPAN - 1)
        for lo in range(0, SUB, LANES):
            lanes = slice(lo, lo + LANES)
            for b in range(spans):
                stack = []
                for k in range(n_rec):
                    tile = jnp.zeros((SPAN, LANES), jnp.float32)
                    for j in range(slots):
                        place = place_ref[slot, k, j, b : b + 1, lanes]
                        value = record_buf[k, i, b * slots + j : b * slots + j + 1, lanes]
                        tile = jnp.where(place == ids, value, tile)
                    stack.append(tile)
                    done = k + 1
                    while done % 2 == 0:
                        right = stack.pop()
                        stack[-1] = stack[-1] + right
                        done //= 2
                tile_refs[slot][b * SPAN : (b + 1) * SPAN, lanes] = stack[0]

    def decode(slot, i):
        decoded = dot_split(basis_ref[2], basis_ref[3], tile_refs[slot][...])
        decoded_buf[i] = decoded
        squares_ref[:, lanes_at(i)] = jnp.sum(decoded * decoded, axis=0, keepdims=True)
        copy_out(i).start()

    def work(tiles):
        for slot, i in enumerate(tiles):
            spread(slot, i)
            decode(slot, i)

    pairs_of(count, work)
    for i in range(count):
        copy_out(i).wait()


def scale_kernel(n_sq, n_all, count, start, *refs):
    decoded_ref, sq_refs = refs[0], refs[1 : 1 + n_sq]
    out_ref, decoded_buf, out_buf, in_sem, out_sem = refs[-5:]

    def copy_in(i):
        return pltpu.make_async_copy(
            decoded_ref.at[:, lanes_at(i)], decoded_buf.at[i], in_sem.at[i]
        )

    def copy_out(i):
        return pltpu.make_async_copy(
            out_buf.at[i], out_ref.at[lanes_at(i, start)], out_sem.at[i]
        )

    for i in range(count):
        copy_in(i).start()

    def step(i, carry):
        total = sq_refs[0][:, lanes_at(i)]
        for ref in sq_refs[1:]:
            total = total + ref[:, lanes_at(i)]
        scale = 1.0 / jnp.sqrt(total * (1.0 / n_all) + 1e-05)
        copy_in(i).wait()
        out_buf[i] = (decoded_buf[i] * scale).astype(jnp.bfloat16).T
        copy_out(i).start()
        return carry

    lax.fori_loop(0, count, step, 0)
    for i in range(count):
        copy_out(i).wait()


def call(kernel, out_shape, n_vmem, scratch, aliases, flops, moved, args):
    vmem = pl.BlockSpec(memory_space=pltpu.VMEM)
    anywhere = pl.BlockSpec(memory_space=pl.ANY)
    many = [anywhere if where == "hbm" else vmem for _, where in out_shape]
    return pl.pallas_call(
        kernel,
        in_specs=[vmem if k in n_vmem else anywhere for k in range(len(args))],
        out_specs=many,
        out_shape=[shape for shape, _ in out_shape],
        scratch_shapes=scratch,
        input_output_aliases=aliases,
        compiler_params=pltpu.CompilerParams(vmem_limit_bytes=VMEM_LIMIT),
        cost_estimate=pl.CostEstimate(flops=flops, bytes_accessed=moved, transcendentals=0),
    )(*args)


def body(momentum, activations, out_grads, positions):
    rows, cols = momentum.shape[1:]
    spans, slots = positions.shape[1:3]
    tokens = activations.shape[0]
    n_tensor, n_dp = lax.axis_size("tensor"), lax.axis_size("dp")
    n_tiles = rows // SUB
    edges = [0]
    for c in CHUNKS:
        edges.append(edges[-1] + c)
    edges = [e * n_tiles // edges[-1] for e in edges]
    basis = jnp.asarray(basis_parts(spans))
    n_rows = spans * slots + spans
    dma = pltpu.SemaphoreType.DMA
    f32, bf16 = jnp.float32, jnp.bfloat16

    line = n_tensor == 4
    if line:
        outer, back = [(0, 1), (3, 2)], [(1, 0), (2, 3)]
        inner = []
        for d in range(n_dp):
            for t, to in ((0, (d ^ 1, 0)), (1, (d, 2)), (2, (d, 1)), (3, (d ^ 1, 3))):
                inner.append((d * n_tensor + t, to[0] * n_tensor + to[1]))
        other_grads = lax.ppermute(out_grads, "tensor", outer)
        owns = []
        for c in range(len(CHUNKS)):
            owns.append(lax.slice_in_dim(activations, edges[c] * SUB, edges[c + 1] * SUB, axis=1))
    else:
        gathered = lax.all_gather(activations, "tensor", axis=0, tiled=True)

    def add_chunk(c, base, group_width, new_momentum, record):
        start, count = edges[c] * SUB, edges[c + 1] - edges[c]
        width = count * SUB
        args = [basis, out_grads, momentum, positions]
        n_act = 4 if line else 1
        if line:
            own = owns[c]
            one = lax.ppermute(own, "tensor", outer)
            two = lax.ppermute(own, ("dp", "tensor"), inner)
            three = lax.ppermute(one, ("dp", "tensor"), inner)
            (coded,) = call(
                functools.partial(partial_kernel, count, start),
                [(jax.ShapeDtypeStruct((cols + 16, width), jnp.int16), "hbm")],
                (0,),
                [
                    pltpu.VMEM((3 * tokens, width), bf16),
                    pltpu.VMEM((cols + 16, width), jnp.int16),
                    pltpu.VMEM((cols, 3 * tokens), bf16),
                    dma((3, count)),
                    dma((count,)),
                ],
                {},
                2 * cols * 3 * tokens * width,
                2 * width * (3 * tokens + cols),
                [other_grads, activations, two, three],
            )
            part = lax.ppermute(coded, "tensor", back)
            args += [activations, one, two, three, part]
        else:
            args += [gathered]
        aliases = {}
        for place, buffer in enumerate((new_momentum, record)):
            if buffer is not None:
                aliases[len(args)] = place
                args.append(buffer)
        return call(
            functools.partial(grad_kernel, n_act, line, slots, count, start, base),
            [
                (jax.ShapeDtypeStruct(momentum.shape, f32), "hbm"),
                (jax.ShapeDtypeStruct((n_rows, group_width), f32), "hbm"),
            ],
            (0, 1),
            [
                pltpu.VMEM((count, SUB, cols), f32),
                pltpu.VMEM((count, spans, slots, SUB), jnp.int32),
                pltpu.VMEM((count, n_tensor * tokens, SUB), bf16),
                pltpu.VMEM((count, cols + 16, SUB), jnp.int16),
                pltpu.VMEM((count, SUB, cols), f32),
                pltpu.VMEM((count, n_rows, SUB), f32),
                pltpu.VMEM((cols, SUB), f32),
                pltpu.VMEM((cols, SUB), f32),
                pltpu.VMEM((cols, SUB), f32),
                pltpu.VMEM((cols, SUB), f32),
                pltpu.VMEM((cols, n_tensor * tokens), bf16),
                dma((n_act + 3, count)),
                dma((2, count)),
            ],
            aliases,
            2 * cols * n_tensor * tokens * width + 12 * cols * cols * width,
            width * (8 * cols + 10 * tokens),
            args,
        )

    new_momentum, update = None, None
    for group in GROUPS:
        base, count = edges[group[0]] * SUB, edges[group[-1] + 1] - edges[group[0]]
        width = count * SUB
        record = None
        for c in group:
            new_momentum, record = add_chunk(c, base, width, new_momentum, record)
        near = [record]
        for k in range(1, n_dp // 2):
            near.append(lax.ppermute(record, "dp", [(i, i ^ (2 * k)) for i in range(n_dp)]))
        records = []
        for r in near:
            records += [r, lax.ppermute(r, "dp", [(i, i ^ 1) for i in range(n_dp)])]
        decoded, squares = call(
            functools.partial(sum_kernel, n_dp, slots, count),
            [
                (jax.ShapeDtypeStruct((cols, width), f32), "hbm"),
                (jax.ShapeDtypeStruct((1, width), f32), "vmem"),
            ],
            (0,),
            [
                pltpu.VMEM((n_dp, count, n_rows, SUB), f32),
                pltpu.VMEM((count, cols, SUB), f32),
                pltpu.VMEM((2, n_dp, slots, spans, SUB), jnp.int32),
                pltpu.VMEM((cols, SUB), f32),
                pltpu.VMEM((cols, SUB), f32),
                dma((n_dp, count)),
                dma((count,)),
            ],
            {},
            6 * cols * cols * width,
            width * 4 * (cols + n_dp * n_rows),
            [basis] + records,
        )
        if line:
            sq_args = [squares]
            for k in range(n_tensor - 1, 0, -1):
                pairs = [(i, i ^ k) for i in range(n_tensor)]
                sq_args.append(lax.ppermute(squares, "tensor", pairs))
        else:
            sq_args = [lax.psum(squares, "tensor")]
        args = [decoded] + sq_args
        aliases = {}
        if update is not None:
            aliases = {len(args): 0}
            args.append(update)
        (update,) = call(
            functools.partial(scale_kernel, len(sq_args), cols * n_tensor, count, base),
            [(jax.ShapeDtypeStruct((rows, cols), bf16), "hbm")],
            range(1, 1 + len(sq_args)),
            [
                pltpu.VMEM((count, cols, SUB), f32),
                pltpu.VMEM((count, SUB, cols), bf16),
                dma((count,)),
                dma((count,)),
            ],
            aliases,
            width * cols,
            width * cols * 6,
            args,
        )
    return new_momentum, update


def solution(mesh):
    placed = (
        P("dp", None, "tensor"),
        P(("dp", "tensor"), None),
        P("dp", "tensor"),
        P("dp", "tensor", None, None),
    )
    return jax.shard_map(
        body,
        mesh=mesh,
        in_specs=placed,
        out_specs=(P("dp", None, "tensor"), P(None, "tensor")),
        check_vma=False,
    )
```

profile of v0, /device:TPU:0, one launch (start us, length us, event | category | flops | bytes accessed | tf_op | source)
XLA Modules:
  0.0 160.5 jit_solution(13849107542215988183)
XLA Ops:
  1.8 5.0 %collective-permute-start.13 = (bf16[128,1536]{1,0:T(8,128)(2,1)S(1)}, bf16[128,1536]{1,0:T(8,128)(2,1)S(1)}, u32[]{:S(2)}, u32[]{:S(2)}) collective-permute-start(bf16[128,1536]{1,0:T(8,128)(2,1)S(1)} %get-tuple-element.26), channel_id=1, source_target_pairs={{0,1},{3,2},{4,5},{7,6},{8,9},{11,10},{12,13},{15,14},{16,17},{19,... | collective-permute-start | bytes 1179656 | tf_op jit(solution)/shard_map/ppermute | solution.py:350
  8.2 8.1 %collective-permute-done.13.refs_5_ = bf16[128,1536]{1,0:T(8,128)(2,1)S(1)} collective-permute-done((bf16[128,1536]{1,0:T(8,128)(2,1)S(1)}, bf16[128,1536]{1,0:T(8,128)(2,1)S(1)}, u32[]{:S(2)}, u32[]{:S(2)}) %collective-permute-start.13) | collective-permute-done | bytes 393248 | tf_op jit(solution)/shard_map/ppermute | solution.py:350
  16.3 6.0 %collective-permute-start.3 = (bf16[512,256]{1,0:T(8,128)(2,1)}, bf16[512,256]{1,0:T(8,128)(2,1)S(1)}, u32[]{:S(2)}, u32[]{:S(2)}) collective-permute-start(bf16[512,256]{1,0:T(8,128)(2,1)} %refs_1_.7), channel_id=1, source_target_pairs={{0,1},{3,2},{4,5},{7,6},{8,9},{11,10},{12,13},{15,14},{16,17},{19,... | collective-permute-start | bytes 786440 | tf_op jit(solution)/shard_map/ppermute | solution.py:336
  22.3 2.4 %collective-permute-done.9.refs_5_ = bf16[128,1536]{1,0:T(8,128)(2,1)S(1)} collective-permute-done((bf16[128,1536]{1,0:T(8,128)(2,1)S(1)}, bf16[128,1536]{1,0:T(8,128)(2,1)S(1)}, u32[]{:S(2)}, u32[]{:S(2)}) %collective-permute-start.9) | collective-permute-done | bytes 393248 | tf_op jit(solution)/shard_map/ppermute | solution.py:350
  24.7 4.6 %collective-permute-done.3.grads_ref = bf16[512,256]{1,0:T(8,128)(2,1)S(1)} collective-permute-done((bf16[512,256]{1,0:T(8,128)(2,1)}, bf16[512,256]{1,0:T(8,128)(2,1)S(1)}, u32[]{:S(2)}, u32[]{:S(2)}) %collective-permute-start.3) | collective-permute-done | bytes 262176 | tf_op jit(solution)/shard_map/ppermute | solution.py:336
  30.6 2.6 %shard_map.71 = s16[272,1536]{1,0:T(8,128)(2,1)S(1)} custom-call(bf16[512,256]{1,0:T(8,128)(2,1)S(1)} %collective-permute-done.3.grads_ref, bf16[128,5120]{1,0:T(8,128)(2,1)S(1)} %copy-done, bf16[128,1536]{1,0:T(8,128)(2,1)S(1)} %collective-permute-done.14.refs_1_.refs_6_, bf16[128,1536]{1,0:T(8,128)(2,1)S(1)} %collective-permute-done.15.refs_2_.refs_7_), custom_call_target="tpu_custom_call" | custom-call | flops 301989888 | bytes 1966080 | tf_op jit(solution)/shard_map/pallas_call | solution.py:302
  34.5 4.6 %collective-permute-start.5 = (bf16[128,1024]{1,0:T(8,128)(2,1)S(1)}, bf16[128,1024]{1,0:T(8,128)(2,1)S(1)}, u32[]{:S(2)}, u32[]{:S(2)}) collective-permute-start(bf16[128,1024]{1,0:T(8,128)(2,1)S(1)} %get-tuple-element.28), channel_id=1, source_target_pairs={{0,1},{3,2},{4,5},{7,6},{8,9},{11,10},{12,13},{15,14},{16,17},{19,... | collective-permute-start | bytes 786440 | tf_op jit(solution)/shard_map/ppermute | solution.py:350
  39.2 2.8 %collective-permute-start = (bf16[128,1024]{1,0:T(8,128)(2,1)S(1)}, bf16[128,1024]{1,0:T(8,128)(2,1)S(1)}, u32[]{:S(2)}, u32[]{:S(2)}) collective-permute-start(bf16[128,1024]{1,0:T(8,128)(2,1)S(1)} %get-tuple-element.29), channel_id=1, source_target_pairs={{0,1},{3,2},{4,5},{7,6},{8,9},{11,10},{12,13},{15,14},{16,17},{19,... | collective-permute-start | bytes 786440 | tf_op jit(solution)/shard_map/ppermute | solution.py:350
  42.1 2.6 %shard_map.70 = s16[272,1536]{1,0:T(8,128)(2,1)S(1)} custom-call(bf16[512,256]{1,0:T(8,128)(2,1)S(1)} %collective-permute-done.3.grads_ref, bf16[128,5120]{1,0:T(8,128)(2,1)S(1)} %copy-done, bf16[128,1536]{1,0:T(8,128)(2,1)S(1)} %collective-permute-done.10.refs_1_.refs_6_, bf16[128,1536]{1,0:T(8,128)(2,1)S(1)} %collective-permute-done.11.refs_2_.refs_7_), custom_call_target="tpu_custom_call" | custom-call | flops 301989888 | bytes 1966080 | tf_op jit(solution)/shard_map/pallas_call | solution.py:302
  46.8 2.4 %collective-permute-done.refs_5_ = bf16[128,1024]{1,0:T(8,128)(2,1)S(1)} collective-permute-done((bf16[128,1024]{1,0:T(8,128)(2,1)S(1)}, bf16[128,1024]{1,0:T(8,128)(2,1)S(1)}, u32[]{:S(2)}, u32[]{:S(2)}) %collective-permute-start) | collective-permute-done | bytes 262176 | tf_op jit(solution)/shard_map/ppermute | solution.py:350
  56.6 7.2 %shard_map.72 = (f32[1,5120,256]{2,1,0:T(8,128)}, f32[20,3072]{1,0:T(8,128)S(1)}) custom-call(bf16[4,256,256]{2,1,0:T(8,128)(2,1)S(1)} %copy-done.3, bf16[512,256]{1,0:T(8,128)(2,1)S(1)} %copy-done.5, f32[1,5120,256]{2,1,0:T(8,128)S(1)} %copy-done.2, s32[1,4,4,5120]{3,2,1,0:T(4,128)S(1)} %copy-done.4, bf16[128,5120]{1,0:T(8,128)(2,1)S(1)} %copy-done.1, ...), custom_call_target="tpu_custom_call" | custom-call | flops 1610612736 | bytes 5111808 | tf_op jit(solution)/shard_map/pallas_call | solution.py:302
  63.8 10.6 %collective-permute-done.12.refs_8_ = s16[272,1536]{1,0:T(8,128)(2,1)S(1)} collective-permute-done((s16[272,1536]{1,0:T(8,128)(2,1)S(1)}, s16[272,1536]{1,0:T(8,128)(2,1)S(1)}, u32[]{:S(2)}, u32[]{:S(2)}) %collective-permute-start.12) | collective-permute-done | bytes 835616 | tf_op jit(solution)/shard_map/ppermute | solution.py:369
  74.5 7.2 %shard_map.73 = (f32[1,5120,256]{2,1,0:T(8,128)}, f32[20,3072]{1,0:T(8,128)S(1)}) custom-call(bf16[4,256,256]{2,1,0:T(8,128)(2,1)S(1)} %copy-done.3, bf16[512,256]{1,0:T(8,128)(2,1)S(1)} %copy-done.5, f32[1,5120,256]{2,1,0:T(8,128)S(1)} %copy-done.2, s32[1,4,4,5120]{3,2,1,0:T(4,128)S(1)} %copy-done.4, ...), custom_call_target="tpu_custom_call", output_to_operand_aliasing={{0}: (9, {}), {1}: (10, {})} | custom-call | flops 1610612736 | bytes 5111808 | tf_op jit(solution)/shard_map/pallas_call | solution.py:302
  86.4 5.2 %shard_map.74 = (f32[1,5120,256]{2,1,0:T(8,128)}, f32[20,2048]{1,0:T(8,128)S(1)}) custom-call(bf16[4,256,256]{2,1,0:T(8,128)(2,1)S(1)} %copy-done.3, bf16[512,256]{1,0:T(8,128)(2,1)S(1)} %copy-done.5, f32[1,5120,256]{2,1,0:T(8,128)S(1)} %copy-done.2, s32[1,4,4,5120]{3,2,1,0:T(4,128)S(1)} %copy-done.4, ...), custom_call_target="tpu_custom_call", output_to_operand_aliasing={{0}: (9, {})} | custom-call | flops 1073741824 | bytes 3407872 | tf_op jit(solution)/shard_map/pallas_call | solution.py:302
  91.6 4.8 %collective-permute-done.4.refs_8_ = s16[272,1024]{1,0:T(8,128)(2,1)S(1)} collective-permute-done((s16[272,1024]{1,0:T(8,128)(2,1)S(1)}, s16[272,1024]{1,0:T(8,128)(2,1)S(1)}, u32[]{:S(2)}, u32[]{:S(2)}) %collective-permute-start.4) | collective-permute-done | bytes 557088 | tf_op jit(solution)/shard_map/ppermute | solution.py:369
  96.4 5.2 %shard_map.75 = (f32[1,5120,256]{2,1,0:T(8,128)}, f32[20,2048]{1,0:T(8,128)S(1)}) custom-call(bf16[4,256,256]{2,1,0:T(8,128)(2,1)S(1)} %copy-done.3, bf16[512,256]{1,0:T(8,128)(2,1)S(1)} %copy-done.5, f32[1,5120,256]{2,1,0:T(8,128)S(1)} %copy-done.2, s32[1,4,4,5120]{3,2,1,0:T(4,128)S(1)} %copy-done.4, ...), custom_call_target="tpu_custom_call", output_to_operand_aliasing={{0}: (9, {}), {1}: (10, {})} | custom-call | flops 1073741824 | bytes 3407872 | tf_op jit(solution)/shard_map/pallas_call | solution.py:302
  104.6 2.7 %collective-permute-done.18.refs_3_ = f32[20,2048]{1,0:T(8,128)S(1)} collective-permute-done((f32[20,2048]{1,0:T(8,128)S(1)}, f32[20,2048]{1,0:T(8,128)S(1)}, u32[]{:S(2)}, u32[]{:S(2)}) %collective-permute-start.18) | collective-permute-done | bytes 163872 | tf_op jit(solution)/shard_map/ppermute | solution.py:415
  108.8 2.0 %collective-permute-start.22 = (f32[20,2048]{1,0:T(8,128)S(1)}, f32[20,2048]{1,0:T(8,128)S(1)}, u32[]{:S(2)}, u32[]{:S(2)}) collective-permute-start(f32[20,2048]{1,0:T(8,128)S(1)} %get-tuple-element.20.refs_1_), channel_id=1, source_target_pairs={{0,24},{4,28},{8,16},{12,20},{16,8},{20,12},{24,0},{28,4},{1,25},{... | collective-permute-start | bytes 491528 | tf_op jit(solution)/shard_map/ppermute | solution.py:415
  110.8 5.3 %collective-permute-done.22.refs_7_ = f32[20,2048]{1,0:T(8,128)S(1)} collective-permute-done((f32[20,2048]{1,0:T(8,128)S(1)}, f32[20,2048]{1,0:T(8,128)S(1)}, u32[]{:S(2)}, u32[]{:S(2)}) %collective-permute-start.22) | collective-permute-done | bytes 163872 | tf_op jit(solution)/shard_map/ppermute | solution.py:415
  117.1 18.0 %shard_map.77 = (f32[256,3072]{1,0:T(8,128)S(1)}, f32[1,3072]{1,0:T(1,128)S(1)}) custom-call(bf16[4,256,256]{2,1,0:T(8,128)(2,1)S(1)} %copy-done.3, f32[20,3072]{1,0:T(8,128)S(1)} %get-tuple-element.23.refs_1_, f32[20,3072]{1,0:T(8,128)S(1)} %collective-permute-done.27.refs_2_, f32[20,3072]{1,0:T(8,128)S(1)} %collective-permute-done.28.refs_3_, ...), custom_call_target="tpu_custom_call" | custom-call | flops 1207959552 | bytes 5111808 | tf_op jit(solution)/shard_map/pallas_call | solution.py:302
  135.1 2.5 %collective-permute-start.34 = (f32[1,3072]{1,0:T(1,128)S(1)}, f32[1,3072]{1,0:T(1,128)S(1)}, u32[]{:S(2)}, u32[]{:S(2)}) collective-permute-start(f32[1,3072]{1,0:T(1,128)S(1)} %get-tuple-element.25.refs_1_), channel_id=1, source_target_pairs={{0,3},{1,2},{2,1},{3,0},{4,7},{5,6},{6,5},{7,4},{8,11},{9,10},{10,... | collective-permute-start | bytes 36872 | tf_op jit(solution)/shard_map/ppermute | solution.py:444
  139.6 11.8 %shard_map.76 = (f32[256,2048]{1,0:T(8,128)S(1)}, f32[1,2048]{1,0:T(1,128)S(1)}) custom-call(bf16[4,256,256]{2,1,0:T(8,128)(2,1)S(1)} %copy-done.3, f32[20,2048]{1,0:T(8,128)S(1)} %get-tuple-element.20.refs_1_, f32[20,2048]{1,0:T(8,128)S(1)} %collective-permute-done.17.refs_2_, f32[20,2048]{1,0:T(8,128)S(1)} %collective-permute-done.18.refs_3_, ...), custom_call_target="tpu_custom_call" | custom-call | flops 805306368 | bytes 3407872 | tf_op jit(solution)/shard_map/pallas_call | solution.py:302
  151.4 2.5 %collective-permute-start.24 = (f32[1,2048]{1,0:T(1,128)S(1)}, f32[1,2048]{1,0:T(1,128)S(1)}, u32[]{:S(2)}, u32[]{:S(2)}) collective-permute-start(f32[1,2048]{1,0:T(1,128)S(1)} %get-tuple-element.22.refs_1_), channel_id=1, source_target_pairs={{0,3},{1,2},{2,1},{3,0},{4,7},{5,6},{6,5},{7,4},{8,11},{9,10},{10,... | collective-permute-start | bytes 24584 | tf_op jit(solution)/shard_map/ppermute | solution.py:444
  155.9 2.5 %shard_map.78.refs_5_ = bf16[5120,256]{1,0:T(8,128)(2,1)} custom-call(f32[256,3072]{1,0:T(8,128)S(1)} %get-tuple-element.24.refs_0_, f32[1,3072]{1,0:T(1,128)S(1)} %get-tuple-element.25.refs_1_, f32[1,3072]{1,0:T(1,128)S(1)} %collective-permute-done.34.refs_2_, f32[1,3072]{1,0:T(1,128)S(1)} %collective-permute-done.35.refs_3_, ...), custom_call_target="tpu_custom_call" | custom-call | flops 786432 | bytes 4718592 | tf_op jit(solution)/shard_map/pallas_call | solution.py:302
  (76 shorter events, 30.8 us)
Async XLA Ops:
  1.8 14.4 %collective-permute-start.13 = (bf16[128,1536]{1,0:T(8,128)(2,1)S(1)}, bf16[128,1536]{1,0:T(8,128)(2,1)S(1)}, u32[]{:S(2)}, u32[]{:S(2)}) collective-permute-start(bf16[128,1536]{1,0:T(8,128)(2,1)S(1)} %get-tuple-element.26), channel_id=1, source_target_pairs={{0,1},{3,2},{4,5},{7,6},{8,9},{11,10},{12,13},{15,14},{16,17},{19,... | collective-permute-start | bytes 1179656 | tf_op jit(solution)/shard_map/ppermute | solution.py:350
  6.8 17.9 %collective-permute-start.9 = (bf16[128,1536]{1,0:T(8,128)(2,1)S(1)}, bf16[128,1536]{1,0:T(8,128)(2,1)S(1)}, u32[]{:S(2)}, u32[]{:S(2)}) collective-permute-start(bf16[128,1536]{1,0:T(8,128)(2,1)S(1)} %get-tuple-element.27), channel_id=1, source_target_pairs={{0,1},{3,2},{4,5},{7,6},{8,9},{11,10},{12,13},{15,14},{16,17},{19,... | collective-permute-start | bytes 1179656 | tf_op jit(solution)/shard_map/ppermute | solution.py:350
  8.1 21.2 %collective-permute-start.14 = (bf16[128,1536]{1,0:T(8,128)(2,1)S(1)}, bf16[128,1536]{1,0:T(8,128)(2,1)S(1)}, u32[]{:S(2)}, u32[]{:S(2)}) collective-permute-start(bf16[128,1536]{1,0:T(8,128)(2,1)S(1)} %get-tuple-element.26), channel_id=1, source_target_pairs={{0,4},{1,2},{2,1},{3,7},{4,0},{5,6},{6,5},{7,3},{8,12},{9,10},{10,... | collective-permute-start | bytes 1179656 | tf_op jit(solution)/shard_map/ppermute | solution.py:351
  16.3 13.0 %collective-permute-start.15 = (bf16[128,1536]{1,0:T(8,128)(2,1)S(1)}, bf16[128,1536]{1,0:T(8,128)(2,1)S(1)}, u32[]{:S(2)}, u32[]{:S(2)}) collective-permute-start(bf16[128,1536]{1,0:T(8,128)(2,1)S(1)} %collective-permute-done.13.refs_5_), channel_id=1, source_target_pairs={{0,4},{1,2},{2,1},{3,7},{4,0},{5,6},{6,5},{7,3},{8,12},{9,10},{10,... | collective-permute-start | bytes 1179656 | tf_op jit(solution)/shard_map/ppermute | solution.py:352
  16.3 13.0 %collective-permute-start.3 = (bf16[512,256]{1,0:T(8,128)(2,1)}, bf16[512,256]{1,0:T(8,128)(2,1)S(1)}, u32[]{:S(2)}, u32[]{:S(2)}) collective-permute-start(bf16[512,256]{1,0:T(8,128)(2,1)} %refs_1_.7), channel_id=1, source_target_pairs={{0,1},{3,2},{4,5},{7,6},{8,9},{11,10},{12,13},{15,14},{16,17},{19,... | collective-permute-start | bytes 786440 | tf_op jit(solution)/shard_map/ppermute | solution.py:336
  22.2 17.0 %collective-permute-start.10 = (bf16[128,1536]{1,0:T(8,128)(2,1)S(1)}, bf16[128,1536]{1,0:T(8,128)(2,1)S(1)}, u32[]{:S(2)}, u32[]{:S(2)}) collective-permute-start(bf16[128,1536]{1,0:T(8,128)(2,1)S(1)} %get-tuple-element.27), channel_id=1, source_target_pairs={{0,4},{1,2},{2,1},{3,7},{4,0},{5,6},{6,5},{7,3},{8,12},{9,10},{10,... | collective-permute-start | bytes 1179656 | tf_op jit(solution)/shard_map/ppermute | solution.py:351
  24.7 17.4 %collective-permute-start.11 = (bf16[128,1536]{1,0:T(8,128)(2,1)S(1)}, bf16[128,1536]{1,0:T(8,128)(2,1)S(1)}, u32[]{:S(2)}, u32[]{:S(2)}) collective-permute-start(bf16[128,1536]{1,0:T(8,128)(2,1)S(1)} %collective-permute-done.9.refs_5_), channel_id=1, source_target_pairs={{0,4},{1,2},{2,1},{3,7},{4,0},{5,6},{6,5},{7,3},{8,12},{9,10},{10,... | collective-permute-start | bytes 1179656 | tf_op jit(solution)/shard_map/ppermute | solution.py:352
  33.2 23.4 %collective-permute-start.16 = (s16[272,1536]{1,0:T(8,128)(2,1)S(1)}, s16[272,1536]{1,0:T(8,128)(2,1)S(1)}, u32[]{:S(2)}, u32[]{:S(2)}) collective-permute-start(s16[272,1536]{1,0:T(8,128)(2,1)S(1)} %shard_map.71), channel_id=1, source_target_pairs={{1,0},{2,3},{5,4},{6,7},{9,8},{10,11},{13,12},{14,15},{17,16},{18,... | collective-permute-start | bytes 2506760 | tf_op jit(solution)/shard_map/ppermute | solution.py:369
  34.5 11.7 %collective-permute-start.5 = (bf16[128,1024]{1,0:T(8,128)(2,1)S(1)}, bf16[128,1024]{1,0:T(8,128)(2,1)S(1)}, u32[]{:S(2)}, u32[]{:S(2)}) collective-permute-start(bf16[128,1024]{1,0:T(8,128)(2,1)S(1)} %get-tuple-element.28), channel_id=1, source_target_pairs={{0,1},{3,2},{4,5},{7,6},{8,9},{11,10},{12,13},{15,14},{16,17},{19,... | collective-permute-start | bytes 786440 | tf_op jit(solution)/shard_map/ppermute | solution.py:350
  39.2 9.9 %collective-permute-start = (bf16[128,1024]{1,0:T(8,128)(2,1)S(1)}, bf16[128,1024]{1,0:T(8,128)(2,1)S(1)}, u32[]{:S(2)}, u32[]{:S(2)}) collective-permute-start(bf16[128,1024]{1,0:T(8,128)(2,1)S(1)} %get-tuple-element.29), channel_id=1, source_target_pairs={{0,1},{3,2},{4,5},{7,6},{8,9},{11,10},{12,13},{15,14},{16,17},{19,... | collective-permute-start | bytes 786440 | tf_op jit(solution)/shard_map/ppermute | solution.py:350
  44.8 29.7 %collective-permute-start.12 = (s16[272,1536]{1,0:T(8,128)(2,1)S(1)}, s16[272,1536]{1,0:T(8,128)(2,1)S(1)}, u32[]{:S(2)}, u32[]{:S(2)}) collective-permute-start(s16[272,1536]{1,0:T(8,128)(2,1)S(1)} %shard_map.70), channel_id=1, source_target_pairs={{1,0},{2,3},{5,4},{6,7},{9,8},{10,11},{13,12},{14,15},{17,16},{18,... | collective-permute-start | bytes 2506760 | tf_op jit(solution)/shard_map/ppermute | solution.py:369
  51.1 35.3 %collective-permute-start.8 = (s16[272,1024]{1,0:T(8,128)(2,1)S(1)}, s16[272,1024]{1,0:T(8,128)(2,1)S(1)}, u32[]{:S(2)}, u32[]{:S(2)}) collective-permute-start(s16[272,1024]{1,0:T(8,128)(2,1)S(1)} %shard_map.69), channel_id=1, source_target_pairs={{1,0},{2,3},{5,4},{6,7},{9,8},{10,11},{13,12},{14,15},{17,16},{18,... | collective-permute-start | bytes 1671176 | tf_op jit(solution)/shard_map/ppermute | solution.py:369
  54.3 42.1 %collective-permute-start.4 = (s16[272,1024]{1,0:T(8,128)(2,1)S(1)}, s16[272,1024]{1,0:T(8,128)(2,1)S(1)}, u32[]{:S(2)}, u32[]{:S(2)}) collective-permute-start(s16[272,1024]{1,0:T(8,128)(2,1)S(1)} %shard_map.68), channel_id=1, source_target_pairs={{1,0},{2,3},{5,4},{6,7},{9,8},{10,11},{13,12},{14,15},{17,16},{18,... | collective-permute-start | bytes 1671176 | tf_op jit(solution)/shard_map/ppermute | solution.py:369
  81.7 25.6 %collective-permute-start.28 = (f32[20,3072]{1,0:T(8,128)S(1)}, f32[20,3072]{1,0:T(8,128)S(1)}, u32[]{:S(2)}, u32[]{:S(2)}) collective-permute-start(f32[20,3072]{1,0:T(8,128)S(1)} %get-tuple-element.23.refs_1_), channel_id=1, source_target_pairs={{0,8},{4,12},{8,0},{12,4},{16,24},{20,28},{24,16},{28,20},{1,9},{5... | collective-permute-start | bytes 737288 | tf_op jit(solution)/shard_map/ppermute | solution.py:415
  83.3 24.5 %collective-permute-start.30 = (f32[20,3072]{1,0:T(8,128)S(1)}, f32[20,3072]{1,0:T(8,128)S(1)}, u32[]{:S(2)}, u32[]{:S(2)}) collective-permute-start(f32[20,3072]{1,0:T(8,128)S(1)} %get-tuple-element.23.refs_1_), channel_id=1, source_target_pairs={{0,16},{4,20},{8,24},{12,28},{16,0},{20,4},{24,8},{28,12},{1,17},{... | collective-permute-start | bytes 737288 | tf_op jit(solution)/shard_map/ppermute | solution.py:415
  84.8 23.1 %collective-permute-start.32 = (f32[20,3072]{1,0:T(8,128)S(1)}, f32[20,3072]{1,0:T(8,128)S(1)}, u32[]{:S(2)}, u32[]{:S(2)}) collective-permute-start(f32[20,3072]{1,0:T(8,128)S(1)} %get-tuple-element.23.refs_1_), channel_id=1, source_target_pairs={{0,24},{4,28},{8,16},{12,20},{16,8},{20,12},{24,0},{28,4},{1,25},{... | collective-permute-start | bytes 737288 | tf_op jit(solution)/shard_map/ppermute | solution.py:415
  107.3 9.3 %collective-permute-start.29 = (f32[20,3072]{1,0:T(8,128)S(1)}, f32[20,3072]{1,0:T(8,128)S(1)}, u32[]{:S(2)}, u32[]{:S(2)}) collective-permute-start(f32[20,3072]{1,0:T(8,128)S(1)} %collective-permute-done.28.refs_3_), channel_id=1, source_target_pairs={{0,4},{4,0},{8,12},{12,8},{16,20},{20,16},{24,28},{28,24},{1,5},{5... | collective-permute-start | bytes 737288 | tf_op jit(solution)/shard_map/ppermute | solution.py:418
  116.1 21.5 %collective-permute-start.17 = (f32[20,2048]{1,0:T(8,128)S(1)}, f32[20,2048]{1,0:T(8,128)S(1)}, u32[]{:S(2)}, u32[]{:S(2)}) collective-permute-start(f32[20,2048]{1,0:T(8,128)S(1)} %get-tuple-element.20.refs_1_), channel_id=1, source_target_pairs={{0,4},{4,0},{8,12},{12,8},{16,20},{20,16},{24,28},{28,24},{1,5},{5... | collective-permute-start | bytes 491528 | tf_op jit(solution)/shard_map/ppermute | solution.py:418
  116.1 21.5 %collective-permute-start.19 = (f32[20,2048]{1,0:T(8,128)S(1)}, f32[20,2048]{1,0:T(8,128)S(1)}, u32[]{:S(2)}, u32[]{:S(2)}) collective-permute-start(f32[20,2048]{1,0:T(8,128)S(1)} %collective-permute-done.18.refs_3_), channel_id=1, source_target_pairs={{0,4},{4,0},{8,12},{12,8},{16,20},{20,16},{24,28},{28,24},{1,5},{5... | collective-permute-start | bytes 491528 | tf_op jit(solution)/shard_map/ppermute | solution.py:418
  116.6 23.0 %collective-permute-start.21 = (f32[20,2048]{1,0:T(8,128)S(1)}, f32[20,2048]{1,0:T(8,128)S(1)}, u32[]{:S(2)}, u32[]{:S(2)}) collective-permute-start(f32[20,2048]{1,0:T(8,128)S(1)} %collective-permute-done.20.refs_5_), channel_id=1, source_target_pairs={{0,4},{4,0},{8,12},{12,8},{16,20},{20,16},{24,28},{28,24},{1,5},{5... | collective-permute-start | bytes 491528 | tf_op jit(solution)/shard_map/ppermute | solution.py:418
  116.7 22.9 %collective-permute-start.23 = (f32[20,2048]{1,0:T(8,128)S(1)}, f32[20,2048]{1,0:T(8,128)S(1)}, u32[]{:S(2)}, u32[]{:S(2)}) collective-permute-start(f32[20,2048]{1,0:T(8,128)S(1)} %collective-permute-done.22.refs_7_), channel_id=1, source_target_pairs={{0,4},{4,0},{8,12},{12,8},{16,20},{20,16},{24,28},{28,24},{1,5},{5... | collective-permute-start | bytes 491528 | tf_op jit(solution)/shard_map/ppermute | solution.py:418
  135.1 18.8 %collective-permute-start.34 = (f32[1,3072]{1,0:T(1,128)S(1)}, f32[1,3072]{1,0:T(1,128)S(1)}, u32[]{:S(2)}, u32[]{:S(2)}) collective-permute-start(f32[1,3072]{1,0:T(1,128)S(1)} %get-tuple-element.25.refs_1_), channel_id=1, source_target_pairs={{0,3},{1,2},{2,1},{3,0},{4,7},{5,6},{6,5},{7,4},{8,11},{9,10},{10,... | collective-permute-start | bytes 36872 | tf_op jit(solution)/shard_map/ppermute | solution.py:444
  137.6 18.2 %collective-permute-start.35 = (f32[1,3072]{1,0:T(1,128)S(1)}, f32[1,3072]{1,0:T(1,128)S(1)}, u32[]{:S(2)}, u32[]{:S(2)}) collective-permute-start(f32[1,3072]{1,0:T(1,128)S(1)} %get-tuple-element.25.refs_1_), channel_id=1, source_target_pairs={{0,2},{1,3},{2,0},{3,1},{4,6},{5,7},{6,4},{7,5},{8,10},{9,11},{10,... | collective-permute-start | bytes 36872 | tf_op jit(solution)/shard_map/ppermute | solution.py:444
  137.7 18.2 %collective-permute-start.36 = (f32[1,3072]{1,0:T(1,128)S(1)}, f32[1,3072]{1,0:T(1,128)S(1)}, u32[]{:S(2)}, u32[]{:S(2)}) collective-permute-start(f32[1,3072]{1,0:T(1,128)S(1)} %get-tuple-element.25.refs_1_), channel_id=1, source_target_pairs={{0,1},{1,0},{2,3},{3,2},{4,5},{5,4},{6,7},{7,6},{8,9},{9,8},{10,11... | collective-permute-start | bytes 36872 | tf_op jit(solution)/shard_map/ppermute | solution.py:444
  (19 other events, 144.2 us)
where the time goes:
time: 161 us
  Pallas kernels  67.8 us (42%)
  starting transfers between devices  45.5 us (28%)
  waiting for transfers between devices  43.4 us (27%)
  local copies, waits for them, and re-layouts  2.56 us (2%)
    pallas_call x12, Pallas kernels, call(): pl.pallas_call(kernel, in_specs=[vmem if k in n_vmem else anywhere for k...  67.8 us
    ppermute x4, waiting for transfers between devices, add_chunk(): part = lax.ppermute(coded, 'tensor', back)  17.4 us
    ppermute x4, starting transfers between devices, add_chunk(): one = lax.ppermute(own, 'tensor', outer)  13.7 us
    ppermute x4, waiting for transfers between devices, add_chunk(): one = lax.ppermute(own, 'tensor', outer)  12.8 us
    ppermute x6, starting transfers between devices, body(): sq_args.append(lax.ppermute(squares, 'tensor', pairs))  8.9 us
    ppermute x6, starting transfers between devices, body(): lax.ppermute(record, 'dp', [(i, i ^ 2 * k) for i in range(n_dp)])  8.62 us
    ppermute x6, waiting for transfers between devices, body(): lax.ppermute(record, 'dp', [(i, i ^ 2 * k) for i in range(n_dp)])  8.45 us
    ppermute x1, starting transfers between devices, body(): other_grads = lax.ppermute(out_grads, 'tensor', outer)  5.96 us
  transfers between devices with their start and end apart: 37, of which 12 were waited for; matrix products, arithmetic and copies ran while one was open for 0% of the time, Pallas kernels for 41%

commit v1 on v0

--- a/solution.py
+++ b/solution.py
@@ -12,32 +12,37 @@
 SPAN = 64
 SUB = 256
 LANES = 128
+SUBLANES = 8
 CODE_TOP = 32764.0
 LN2 = 0.6931471805599453
 VMEM_LIMIT = 40 * 1024 * 1024
-CHUNKS = (6, 6, 4, 4)
-GROUPS = ((0, 1), (2, 3))
-
-
-def basis_parts(spans):
+CHUNKS = (4, 4, 6, 6)
+GROUPS = ((0, 1), (2,), (3,))
+
+
+def basis_parts():
     freq = np.arange(SPAN, dtype=np.float64)[:, None]
     place = np.arange(SPAN, dtype=np.float64)[None, :]
     scales = np.where(freq == 0, (1.0 / SPAN) ** 0.5, (2.0 / SPAN) ** 0.5)
     table = scales * np.cos(np.pi * (2.0 * place + 1.0) * freq / (2 * SPAN))
-    whole = np.kron(np.eye(spans), table).astype(np.float32)
-    high = whole.astype(jnp.bfloat16)
-    low = (whole - high.astype(np.float32)).astype(jnp.bfloat16)
-    return np.stack([high, low, high.T, low.T])
+    table = table.astype(np.float32)
+    high = table.astype(jnp.bfloat16)
+    low = (table - high.astype(np.float32)).astype(jnp.bfloat16)
+    return np.stack([np.concatenate(p, axis=1) for p in ((high, high, low), (high.T, high.T, low.T))])
 
 
 def dot32(a, b):
     return lax.dot_general(a, b, (((1,), (0,)), ((), ())), preferred_element_type=jnp.float32)
 
 
-def dot_split(high, low, x):
-    x_high = x.astype(jnp.bfloat16)
-    x_low = (x - x_high.astype(jnp.float32)).astype(jnp.bfloat16)
-    return dot32(high, x_high) + (dot32(high, x_low) + dot32(low, x_high))
+def dot_split(triple, x):
+    high = x.astype(jnp.bfloat16)
+    low = (x - high.astype(jnp.float32)).astype(jnp.bfloat16)
+    outs = []
+    for at in range(0, x.shape[0], SPAN):
+        part = high[at : at + SPAN]
+        outs.append(dot32(triple, jnp.concatenate([part, low[at : at + SPAN], part], axis=0)))
+    return jnp.concatenate(outs, axis=0)
 
 
 def lanes_at(i, offset=0):
@@ -57,10 +62,9 @@
 
 
 def pairs_of(count, work):
-    if count % 2 == 0:
-        lax.fori_loop(0, count // 2, lambda i, c: work((2 * i, 2 * i + 1)), None)
-    else:
-        lax.fori_loop(0, count, lambda i, c: work((i,)), None)
+    lax.fori_loop(0, count // 2, lambda i, c: work((2 * i, 2 * i + 1)), None)
+    if count % 2:
+        work((count - 1,))
 
 
 def partial_kernel(count, start, grads_ref, *refs):
@@ -118,7 +122,7 @@
     cols = moment_ref.shape[2]
     spans = cols // SPAN
     tokens = act_refs[0].shape[0]
-    ids = lax.broadcasted_iota(jnp.int32, (SPAN, LANES), 0)
+    ids = lax.broadcasted_iota(jnp.int32, (SUBLANES, LANES), 0)
 
     def copies_in(i):
         pairs = [
@@ -161,29 +165,35 @@
             level = part_buf[i, cols:][:1].astype(jnp.int32).astype(jnp.float32)
             code = part_buf[i, :cols].astype(jnp.int32).astype(jnp.float32)
             total = total + code * (jnp.exp(level * LN2) * (1.0 / CODE_TOP))
-        coeffs_ref[...] = dot_split(basis_ref[0], basis_ref[1], total)
+        coeffs_ref[...] = dot_split(basis_ref[0], total)
         return total
 
     def pick(i, coeffs_ref, tile_ref):
         for lo in range(0, SUB, LANES):
             lanes = slice(lo, lo + LANES)
             for b in range(spans):
-                block = coeffs_ref[b * SPAN : (b + 1) * SPAN, lanes]
-                tile = jnp.zeros_like(block)
+                rows = [b * SPAN + h * SUBLANES for h in range(SPAN // SUBLANES)]
+                blocks = [coeffs_ref[at : at + SUBLANES, lanes] for at in rows]
+                parts = [jnp.zeros((SUBLANES, LANES), jnp.float32)] * len(rows)
                 code = jnp.zeros((1, LANES), jnp.int32)
                 for j in range(slots):
                     place = picks_buf[i, b, j : j + 1, lanes]
-                    hit = place == ids
-                    value = jnp.sum(jnp.where(hit, block, 0.0), axis=0, keepdims=True)
-                    tile = jnp.where(hit, block, tile)
+                    offset = place - ids
+                    value = jnp.zeros((SUBLANES, LANES), jnp.float32)
+                    for h in range(len(rows)):
+                        hit = offset == h * SUBLANES
+                        value = jnp.where(hit, blocks[h], value)
+                        parts[h] = jnp.where(hit, blocks[h], parts[h])
+                    value = jnp.sum(value, axis=0, keepdims=True)
                     record_buf[i, b * slots + j : b * slots + j + 1, lanes] = value
                     code = code + place * SPAN**j
-                tile_ref[b * SPAN : (b + 1) * SPAN, lanes] = tile
+                for at, part in zip(rows, parts):
+                    tile_ref[at : at + SUBLANES, lanes] = part
                 row = spans * slots + b
                 record_buf[i, row : row + 1, lanes] = code.astype(jnp.float32)
 
     def finish(i, total, tile_ref):
-        restored = dot_split(basis_ref[2], basis_ref[3], tile_ref[...])
+        restored = dot_split(basis_ref[1], tile_ref[...])
         new_buf[i] = (total - restored).T
         for copy in copies_out(i):
             copy.start()
@@ -200,23 +210,27 @@
             copy.wait()
 
 
-def sum_kernel(n_rec, slots, count, *refs):
+def tile_of(i, split, ahead=0):
+    return i * split + (lax.axis_index("dp") + ahead) % split
+
+
+def sum_kernel(n_rec, slots, count, base, split, *refs):
     basis_ref = refs[0]
     record_refs = refs[1 : 1 + n_rec]
-    decoded_ref, squares_ref, record_buf, decoded_buf = refs[1 + n_rec : 5 + n_rec]
-    place_ref, tile_refs, in_sem, out_sem = refs[5 + n_rec], refs[6 + n_rec : 8 + n_rec], *refs[8 + n_rec :]
+    decoded_ref, squares_ref, record_buf, decoded_buf, place_ref = refs[-9:-4]
+    tile_refs, in_sem, out_sem = refs[-4:-2], *refs[-2:]
     cols = decoded_ref.shape[0]
     spans = cols // SPAN
-    ids = lax.broadcasted_iota(jnp.int32, (SPAN, LANES), 0)
+    ids = lax.broadcasted_iota(jnp.int32, (SUBLANES, LANES), 0)
 
     def copy_in(k, i):
         return pltpu.make_async_copy(
-            record_refs[k].at[:, lanes_at(i)], record_buf.at[k, i], in_sem.at[k, i]
+            record_refs[k].at[:, lanes_at(tile_of(i, split))], record_buf.at[k, i], in_sem.at[k, i]
         )
 
     def copy_out(i):
         return pltpu.make_async_copy(
-            decoded_buf.at[i], decoded_ref.at[:, lanes_at(i)], out_sem.at[i]
+            decoded_buf.at[i], decoded_ref.at[:, lanes_at(i, base)], out_sem.at[i]
         )
 
     for i in range(count):
@@ -234,21 +248,25 @@
             for b in range(spans):
                 stack = []
                 for k in range(n_rec):
-                    tile = jnp.zeros((SPAN, LANES), jnp.float32)
+                    parts = [jnp.zeros((SUBLANES, LANES), jnp.float32)] * (SPAN // SUBLANES)
                     for j in range(slots):
-                        place = place_ref[slot, k, j, b : b + 1, lanes]
+                        place = place_ref[slot, k, j, b : b + 1, lanes] - ids
                         value = record_buf[k, i, b * slots + j : b * slots + j + 1, lanes]
-                        tile = jnp.where(place == ids, value, tile)
-                    stack.append(tile)
+                        value = jnp.broadcast_to(value, (SUBLANES, LANES))
+                        for h in range(SPAN // SUBLANES):
+                            parts[h] = jnp.where(place == h * SUBLANES, value, parts[h])
+                    stack.append(parts)
                     done = k + 1
                     while done % 2 == 0:
                         right = stack.pop()
-                        stack[-1] = stack[-1] + right
+                        stack[-1] = [x + y for x, y in zip(stack[-1], right)]
                         done //= 2
-                tile_refs[slot][b * SPAN : (b + 1) * SPAN, lanes] = stack[0]
+                for h, part in enumerate(stack[0]):
+                    at = b * SPAN + h * SUBLANES
+                    tile_refs[slot][at : at + SUBLANES, lanes] = part
 
     def decode(slot, i):
-        decoded = dot_split(basis_ref[2], basis_ref[3], tile_refs[slot][...])
+        decoded = dot_split(basis_ref[1], tile_refs[slot][...])
         decoded_buf[i] = decoded
         squares_ref[:, lanes_at(i)] = jnp.sum(decoded * decoded, axis=0, keepdims=True)
         copy_out(i).start()
@@ -263,9 +281,9 @@
         copy_out(i).wait()
 
 
-def scale_kernel(n_sq, n_all, count, start, *refs):
+def scale_kernel(n_sq, n_all, count, split, *refs):
     decoded_ref, sq_refs = refs[0], refs[1 : 1 + n_sq]
-    out_ref, decoded_buf, out_buf, in_sem, out_sem = refs[-5:]
+    out_ref, half_ref, decoded_buf, in_sem, out_sem = refs[-5:]
 
     def copy_in(i):
         return pltpu.make_async_copy(
@@ -274,7 +292,7 @@
 
     def copy_out(i):
         return pltpu.make_async_copy(
-            out_buf.at[i], out_ref.at[lanes_at(i, start)], out_sem.at[i]
+            half_ref.at[i], out_ref.at[lanes_at(tile_of(i, split))], out_sem.at[i]
         )
 
     for i in range(count):
@@ -286,11 +304,23 @@
             total = total + ref[:, lanes_at(i)]
         scale = 1.0 / jnp.sqrt(total * (1.0 / n_all) + 1e-05)
         copy_in(i).wait()
-        out_buf[i] = (decoded_buf[i] * scale).astype(jnp.bfloat16).T
+        half_ref[i] = (decoded_buf[i] * scale).astype(jnp.bfloat16).T
         copy_out(i).start()
         return carry
 
     lax.fori_loop(0, count, step, 0)
+    for i in range(count):
+        copy_out(i).wait()
+
+
+def place_kernel(count, split, half_ref, update_ref, out_ref, out_sem):
+    def copy_out(i):
+        return pltpu.make_async_copy(
+            half_ref.at[i], out_ref.at[lanes_at(tile_of(i, split, 1))], out_sem.at[i]
+        )
+
+    for i in range(count):
+        copy_out(i).start()
     for i in range(count):
         copy_out(i).wait()
 
@@ -321,7 +351,7 @@
     for c in CHUNKS:
         edges.append(edges[-1] + c)
     edges = [e * n_tiles // edges[-1] for e in edges]
-    basis = jnp.asarray(basis_parts(spans))
+    basis = jnp.asarray(basis_parts())
     n_rows = spans * slots + spans
     dma = pltpu.SemaphoreType.DMA
     f32, bf16 = jnp.float32, jnp.bfloat16
@@ -403,7 +433,9 @@
             args,
         )
 
-    new_momentum, update = None, None
+    counts = [edges[group[-1] + 1] - edges[group[0]] for group in GROUPS]
+    split = 2 if n_dp % 2 == 0 and all(n % 2 == 0 for n in counts) else 1
+    new_momentum, decoded, square_list = None, None, []
     for group in GROUPS:
         base, count = edges[group[0]] * SUB, edges[group[-1] + 1] - edges[group[0]]
         width = count * SUB
@@ -413,56 +445,68 @@
         near = [record]
         for k in range(1, n_dp // 2):
             near.append(lax.ppermute(record, "dp", [(i, i ^ (2 * k)) for i in range(n_dp)]))
-        records = []
+        args = [basis]
         for r in near:
-            records += [r, lax.ppermute(r, "dp", [(i, i ^ 1) for i in range(n_dp)])]
+            args += [r, lax.ppermute(r, "dp", [(i, i ^ 1) for i in range(n_dp)])]
+        aliases = {}
+        if decoded is not None:
+            aliases = {len(args): 0}
+            args.append(decoded)
         decoded, squares = call(
-            functools.partial(sum_kernel, n_dp, slots, count),
+            functools.partial(sum_kernel, n_dp, slots, count // split, base // split, split),
             [
-                (jax.ShapeDtypeStruct((cols, width), f32), "hbm"),
-                (jax.ShapeDtypeStruct((1, width), f32), "vmem"),
+                (jax.ShapeDtypeStruct((cols, rows // split), f32), "hbm"),
+                (jax.ShapeDtypeStruct((1, width // split), f32), "vmem"),
             ],
             (0,),
             [
-                pltpu.VMEM((n_dp, count, n_rows, SUB), f32),
-                pltpu.VMEM((count, cols, SUB), f32),
+                pltpu.VMEM((n_dp, count // split, n_rows, SUB), f32),
+                pltpu.VMEM((count // split, cols, SUB), f32),
                 pltpu.VMEM((2, n_dp, slots, spans, SUB), jnp.int32),
                 pltpu.VMEM((cols, SUB), f32),
                 pltpu.VMEM((cols, SUB), f32),
-                dma((n_dp, count)),
-                dma((count,)),
+                dma((n_dp, count // split)),
+                dma((count // split,)),
             ],
-            {},
+            aliases,
             6 * cols * cols * width,
             width * 4 * (cols + n_dp * n_rows),
-            [basis] + records,
-        )
-        if line:
-            sq_args = [squares]
-            for k in range(n_tensor - 1, 0, -1):
-                pairs = [(i, i ^ k) for i in range(n_tensor)]
-                sq_args.append(lax.ppermute(squares, "tensor", pairs))
-        else:
-            sq_args = [lax.psum(squares, "tensor")]
-        args = [decoded] + sq_args
-        aliases = {}
-        if update is not None:
-            aliases = {len(args): 0}
-            args.append(update)
+            args,
+        )
+        square_list.append(squares)
+    squares = jnp.concatenate(square_list, axis=1)
+    if line:
+        sq_args = [squares]
+        for k in range(n_tensor - 1, 0, -1):
+            pairs = [(i, i ^ k) for i in range(n_tensor)]
+            sq_args.append(lax.ppermute(squares, "tensor", pairs))
+    else:
+        sq_args = [lax.psum(squares, "tensor")]
+    n_mine = n_tiles // split
+    update, half = call(
+        functools.partial(scale_kernel, len(sq_args), cols * n_tensor, n_mine, split),
+        [
+            (jax.ShapeDtypeStruct((rows, cols), bf16), "hbm"),
+            (jax.ShapeDtypeStruct((n_mine, SUB, cols), bf16), "vmem"),
+        ],
+        range(1, 1 + len(sq_args)),
+        [pltpu.VMEM((n_mine, cols, SUB), f32), dma((n_mine,)), dma((n_mine,))],
+        {},
+        rows * cols,
+        rows * cols * 6,
+        [decoded] + sq_args,
+    )
+    if split == 2:
+        half = lax.ppermute(half, "dp", [(i, i ^ 1) for i in range(n_dp)])
         (update,) = call(
-            functools.partial(scale_kernel, len(sq_args), cols * n_tensor, count, base),
+            functools.partial(place_kernel, n_mine, split),
             [(jax.ShapeDtypeStruct((rows, cols), bf16), "hbm")],
-            range(1, 1 + len(sq_args)),
-            [
-                pltpu.VMEM((count, cols, SUB), f32),
-                pltpu.VMEM((count, SUB, cols), bf16),
-                dma((count,)),
-                dma((count,)),
-            ],
-            aliases,
-            width * cols,
-            width * cols * 6,
-            args,
+            (0,),
+            [dma((n_mine,))],
+            {1: 0},
+            rows * cols,
+            rows * cols * 2,
+            [half, update],
         )
     return new_momentum, update
 

time: 161 us -> 169 us (1.050)
  waiting for transfers between devices: 43.4 us -> 77.6 us
  Pallas kernels: 67.8 us -> 45.5 us
  starting transfers between devices: 45.5 us -> 41.8 us
    ppermute x4, waiting for transfers between devices: 17.4 us -> 40.8 us  [add_chunk(): part = lax.ppermute(coded, 'tensor', back)]
    pallas_call x12 -> x13, Pallas kernels: 67.8 us -> 45.5 us  [call(): pl.pallas_call(kernel, in_specs=[vmem if k in n_vmem else anywhere for k...]
    ppermute x6 -> x3, starting transfers between devices: 8.9 us -> 4.45 us  [body(): sq_args.append(lax.ppermute(squares, 'tensor', pairs))]
    ppermute x1, waiting for transfers between devices: 4.59 us -> 7.87 us  [body(): other_grads = lax.ppermute(out_grads, 'tensor', outer)]
    ppermute x1, starting transfers between devices: 5.96 us -> 2.81 us  [body(): other_grads = lax.ppermute(out_grads, 'tensor', outer)]
    ppermute x8 -> x13, waiting for transfers between devices: 0.02 us -> 3.05 us  [the longest x1 3.02 us: body(): half = lax.ppermute(half, 'dp', [(i, i ^ 1) for i in range(n_dp)])]
    ppermute x6 -> x9, starting transfers between devices: 8.62 us -> 11.6 us  [body(): lax.ppermute(record, 'dp', [(i, i ^ 2 * k) for i in range(n_dp)])]
    ppermute x6 -> x3, waiting for transfers between devices: 0.16 us -> 2.66 us  [body(): sq_args.append(lax.ppermute(squares, 'tensor', pairs))]
  transfers between devices with their start and end apart: 37 -> 42, of which waited for: 12 -> 11; matrix products, arithmetic and copies ran while one was open for 0% -> 1% of each run, Pallas kernels for 41% -> 23%
where the time goes in v1:
time: 169 us
  waiting for transfers between devices  77.6 us (46%)
  Pallas kernels  45.5 us (27%)
  starting transfers between devices  41.8 us (25%)
  local copies, waits for them, and re-layouts  2.56 us (2%)
    pallas_call x13, Pallas kernels, call(): pl.pallas_call(kernel, in_specs=[vmem if k in n_vmem else anywhere for k...  45.5 us
    ppermute x4, waiting for transfers between devices, add_chunk(): part = lax.ppermute(coded, 'tensor', back)  40.8 us
    ppermute x4, starting transfers between devices, add_chunk(): one = lax.ppermute(own, 'tensor', outer)  13.4 us
    ppermute x4, waiting for transfers between devices, add_chunk(): one = lax.ppermute(own, 'tensor', outer)  12.4 us
    ppermute x9, starting transfers between devices, body(): lax.ppermute(record, 'dp', [(i, i ^ 2 * k) for i in range(n_dp)])  11.6 us
    ppermute x9, waiting for transfers between devices, body(): lax.ppermute(record, 'dp', [(i, i ^ 2 * k) for i in range(n_dp)])  10.8 us
    ppermute x1, waiting for transfers between devices, body(): other_grads = lax.ppermute(out_grads, 'tensor', outer)  7.87 us
    ppermute x4, starting transfers between devices, add_chunk(): part = lax.ppermute(coded, 'tensor', back)  5.61 us
  transfers between devices with their start and end apart: 42, of which 11 were waited for; matrix products, arithmetic and copies ran while one was open for 1% of the time, Pallas kernels for 23%

profile of v1, /device:TPU:0, one launch (start us, length us, event | category | flops | bytes accessed | tf_op | source)
XLA Modules:
  0.0 168.8 jit_solution(17930374186649436951)
XLA Ops:
  1.8 5.0 %collective-permute-start.13 = (bf16[128,1024]{1,0:T(8,128)(2,1)S(1)}, bf16[128,1024]{1,0:T(8,128)(2,1)S(1)}, u32[]{:S(2)}, u32[]{:S(2)}) collective-permute-start(bf16[128,1024]{1,0:T(8,128)(2,1)S(1)} %get-tuple-element.34), channel_id=1, source_target_pairs={{0,1},{3,2},{4,5},{7,6},{8,9},{11,10},{12,13},{15,14},{16,17},{19,... | collective-permute-start | bytes 786440 | tf_op jit(solution)/shard_map/ppermute | solution.py:380
  9.7 2.8 %collective-permute-start.3 = (bf16[512,256]{1,0:T(8,128)(2,1)S(1)}, bf16[512,256]{1,0:T(8,128)(2,1)S(1)}, u32[]{:S(2)}, u32[]{:S(2)}) collective-permute-start(bf16[512,256]{1,0:T(8,128)(2,1)S(1)} %copy-done.2), channel_id=1, source_target_pairs={{0,1},{3,2},{4,5},{7,6},{8,9},{11,10},{12,13},{15,14},{16,17},{19,... | collective-permute-start | bytes 786440 | tf_op jit(solution)/shard_map/ppermute | solution.py:366
  13.9 5.7 %collective-permute-start.9 = (bf16[128,1024]{1,0:T(8,128)(2,1)S(1)}, bf16[128,1024]{1,0:T(8,128)(2,1)S(1)}, u32[]{:S(2)}, u32[]{:S(2)}) collective-permute-start(bf16[128,1024]{1,0:T(8,128)(2,1)S(1)} %get-tuple-element.35), channel_id=1, source_target_pairs={{0,1},{3,2},{4,5},{7,6},{8,9},{11,10},{12,13},{15,14},{16,17},{19,... | collective-permute-start | bytes 786440 | tf_op jit(solution)/shard_map/ppermute | solution.py:380
  19.6 7.9 %collective-permute-done.3.grads_ref = bf16[512,256]{1,0:T(8,128)(2,1)S(1)} collective-permute-done((bf16[512,256]{1,0:T(8,128)(2,1)S(1)}, bf16[512,256]{1,0:T(8,128)(2,1)S(1)}, u32[]{:S(2)}, u32[]{:S(2)}) %collective-permute-start.3) | collective-permute-done | bytes 262176 | tf_op jit(solution)/shard_map/ppermute | solution.py:366
  28.0 12.4 %collective-permute-done.9.refs_5_ = bf16[128,1024]{1,0:T(8,128)(2,1)S(1)} collective-permute-done((bf16[128,1024]{1,0:T(8,128)(2,1)S(1)}, bf16[128,1024]{1,0:T(8,128)(2,1)S(1)}, u32[]{:S(2)}, u32[]{:S(2)}) %collective-permute-start.9) | collective-permute-done | bytes 262176 | tf_op jit(solution)/shard_map/ppermute | solution.py:380
  44.8 2.6 %shard_map.69 = s16[272,1536]{1,0:T(8,128)(2,1)S(1)} custom-call(bf16[512,256]{1,0:T(8,128)(2,1)S(1)} %collective-permute-done.3.grads_ref, bf16[128,5120]{1,0:T(8,128)(2,1)S(1)} %copy-done, bf16[128,1536]{1,0:T(8,128)(2,1)S(1)} %collective-permute-done.6.refs_1_.refs_6_, bf16[128,1536]{1,0:T(8,128)(2,1)S(1)} %collective-permute-done.7.refs_2_.refs_7_), custom_call_target="tpu_custom_call" | custom-call | flops 301989888 | bytes 1966080 | tf_op jit(solution)/shard_map/pallas_call | solution.py:332
  52.1 2.6 %shard_map.68 = s16[272,1536]{1,0:T(8,128)(2,1)S(1)} custom-call(bf16[512,256]{1,0:T(8,128)(2,1)S(1)} %collective-permute-done.3.grads_ref, bf16[128,5120]{1,0:T(8,128)(2,1)S(1)} %copy-done, bf16[128,1536]{1,0:T(8,128)(2,1)S(1)} %collective-permute-done.1.refs_1_.refs_6_, bf16[128,1536]{1,0:T(8,128)(2,1)S(1)} %collective-permute-done.2.refs_2_.refs_7_), custom_call_target="tpu_custom_call" | custom-call | flops 301989888 | bytes 1966080 | tf_op jit(solution)/shard_map/pallas_call | solution.py:332
  56.2 4.8 %collective-permute-done.16.refs_8_ = s16[272,1024]{1,0:T(8,128)(2,1)S(1)} collective-permute-done((s16[272,1024]{1,0:T(8,128)(2,1)S(1)}, s16[272,1024]{1,0:T(8,128)(2,1)S(1)}, u32[]{:S(2)}, u32[]{:S(2)}) %collective-permute-start.16) | collective-permute-done | bytes 557088 | tf_op jit(solution)/shard_map/ppermute | solution.py:399
  61.0 4.6 %shard_map.72 = (f32[1,5120,256]{2,1,0:T(8,128)}, f32[20,2048]{1,0:T(8,128)S(1)}) custom-call(bf16[2,64,192]{2,1,0:T(8,128)(2,1)S(1)} %copy-done.3, bf16[512,256]{1,0:T(8,128)(2,1)S(1)} %copy-done.2, f32[1,5120,256]{2,1,0:T(8,128)S(1)} %bitcast.1, s32[1,4,4,5120]{3,2,1,0:T(4,128)S(1)} %copy-done.1, bf16[128,5120]{1,0:T(8,128)(2,1)S(1)} %copy-done, ...), custom_call_target="tpu_custom_call" | custom-call | flops 1073741824 | bytes 3407872 | tf_op jit(solution)/shard_map/pallas_call | solution.py:332
  65.6 36.0 %collective-permute-done.12.refs_8_ = s16[272,1024]{1,0:T(8,128)(2,1)S(1)} collective-permute-done((s16[272,1024]{1,0:T(8,128)(2,1)S(1)}, s16[272,1024]{1,0:T(8,128)(2,1)S(1)}, u32[]{:S(2)}, u32[]{:S(2)}) %collective-permute-start.12) | collective-permute-done | bytes 557088 | tf_op jit(solution)/shard_map/ppermute | solution.py:399
  101.6 4.6 %shard_map.73 = (f32[1,5120,256]{2,1,0:T(8,128)}, f32[20,2048]{1,0:T(8,128)S(1)}) custom-call(bf16[2,64,192]{2,1,0:T(8,128)(2,1)S(1)} %copy-done.3, bf16[512,256]{1,0:T(8,128)(2,1)S(1)} %copy-done.2, f32[1,5120,256]{2,1,0:T(8,128)S(1)} %bitcast.1, s32[1,4,4,5120]{3,2,1,0:T(4,128)S(1)} %copy-done.1, ...), custom_call_target="tpu_custom_call", output_to_operand_aliasing={{0}: (9, {}), {1}: (10, {})} | custom-call | flops 1073741824 | bytes 3407872 | tf_op jit(solution)/shard_map/pallas_call | solution.py:332
  109.8 2.2 %collective-permute-done.32.refs_3_ = f32[20,2048]{1,0:T(8,128)S(1)} collective-permute-done((f32[20,2048]{1,0:T(8,128)S(1)}, f32[20,2048]{1,0:T(8,128)S(1)}, u32[]{:S(2)}, u32[]{:S(2)}) %collective-permute-start.32) | collective-permute-done | bytes 163872 | tf_op jit(solution)/shard_map/ppermute | solution.py:447
  111.9 2.7 %collective-permute-done.34.refs_5_ = f32[20,2048]{1,0:T(8,128)S(1)} collective-permute-done((f32[20,2048]{1,0:T(8,128)S(1)}, f32[20,2048]{1,0:T(8,128)S(1)}, u32[]{:S(2)}, u32[]{:S(2)}) %collective-permute-start.34) | collective-permute-done | bytes 163872 | tf_op jit(solution)/shard_map/ppermute | solution.py:447
  116.4 6.4 %shard_map.74 = (f32[1,5120,256]{2,1,0:T(8,128)}, f32[20,1536]{1,0:T(8,128)S(1)}) custom-call(bf16[2,64,192]{2,1,0:T(8,128)(2,1)S(1)} %copy-done.3, bf16[512,256]{1,0:T(8,128)(2,1)S(1)} %copy-done.2, f32[1,5120,256]{2,1,0:T(8,128)S(1)} %bitcast.1, s32[1,4,4,5120]{3,2,1,0:T(4,128)S(1)} %copy-done.1, ...), custom_call_target="tpu_custom_call", output_to_operand_aliasing={{0}: (9, {})} | custom-call | flops 1610612736 | bytes 5111808 | tf_op jit(solution)/shard_map/pallas_call | solution.py:332
  123.5 6.4 %shard_map.75 = (f32[1,5120,256]{2,1,0:T(8,128)}, f32[20,1536]{1,0:T(8,128)S(1)}) custom-call(bf16[2,64,192]{2,1,0:T(8,128)(2,1)S(1)} %copy-done.3, bf16[512,256]{1,0:T(8,128)(2,1)S(1)} %copy-done.2, f32[1,5120,256]{2,1,0:T(8,128)S(1)} %bitcast.1, s32[1,4,4,5120]{3,2,1,0:T(4,128)S(1)} %copy-done.1, ...), custom_call_target="tpu_custom_call", output_to_operand_aliasing={{0}: (9, {})} | custom-call | flops 1610612736 | bytes 5111808 | tf_op jit(solution)/shard_map/pallas_call | solution.py:332
  134.7 4.7 %collective-permute-done.27.refs_5_ = f32[20,1536]{1,0:T(8,128)S(1)} collective-permute-done((f32[20,1536]{1,0:T(8,128)S(1)}, f32[20,1536]{1,0:T(8,128)S(1)}, u32[]{:S(2)}, u32[]{:S(2)}) %collective-permute-start.27) | collective-permute-done | bytes 122912 | tf_op jit(solution)/shard_map/ppermute | solution.py:447
  139.4 2.5 %collective-permute-start.22 = (f32[20,1536]{1,0:T(8,128)S(1)}, f32[20,1536]{1,0:T(8,128)S(1)}, u32[]{:S(2)}, u32[]{:S(2)}) collective-permute-start(f32[20,1536]{1,0:T(8,128)S(1)} %get-tuple-element.23.refs_1_), channel_id=1, source_target_pairs={{0,24},{4,28},{8,16},{12,20},{16,8},{20,12},{24,0},{28,4},{1,25},{... | collective-permute-start | bytes 368648 | tf_op jit(solution)/shard_map/ppermute | solution.py:447
  142.5 4.3 %shard_map.76 = (f32[256,2560]{1,0:T(8,128)S(1)}, f32[1,1024]{1,0:T(1,128)S(1)}) custom-call(bf16[2,64,192]{2,1,0:T(8,128)(2,1)S(1)} %copy-done.3, f32[20,2048]{1,0:T(8,128)S(1)} %get-tuple-element.25.refs_1_, f32[20,2048]{1,0:T(8,128)S(1)} %collective-permute-done.31.refs_2_, f32[20,2048]{1,0:T(8,128)S(1)} %collective-permute-done.32.refs_3_, ...), custom_call_target="tpu_custom_call" | custom-call | flops 805306368 | bytes 3407872 | tf_op jit(solution)/shard_map/pallas_call | solution.py:332
  148.0 3.6 %shard_map.77 = (f32[256,2560]{1,0:T(8,128)S(1)}, f32[1,768]{1,0:T(1,128)S(1)}) custom-call(bf16[2,64,192]{2,1,0:T(8,128)(2,1)S(1)} %copy-done.3, f32[20,1536]{1,0:T(8,128)S(1)} %get-tuple-element.24.refs_1_, f32[20,1536]{1,0:T(8,128)S(1)} %collective-permute-done.24.refs_2_, ...), custom_call_target="tpu_custom_call", output_to_operand_aliasing={{0}: (9, {})} | custom-call | flops 603979776 | bytes 2555904 | tf_op jit(solution)/shard_map/pallas_call | solution.py:332
  151.7 3.4 %shard_map.78 = (f32[256,2560]{1,0:T(8,128)S(1)}, f32[1,768]{1,0:T(1,128)S(1)}) custom-call(bf16[2,64,192]{2,1,0:T(8,128)(2,1)S(1)} %copy-done.3, f32[20,1536]{1,0:T(8,128)S(1)} %get-tuple-element.23.refs_1_, f32[20,1536]{1,0:T(8,128)S(1)} %collective-permute-done.17.refs_2_, ...), custom_call_target="tpu_custom_call", output_to_operand_aliasing={{0}: (9, {})} | custom-call | flops 603979776 | bytes 2555904 | tf_op jit(solution)/shard_map/pallas_call | solution.py:332
  155.1 2.5 %collective-permute-start.38 = (f32[1,2560]{1,0:T(1,128)S(1)}, f32[1,2560]{1,0:T(1,128)S(1)}, u32[]{:S(2)}, u32[]{:S(2)}) collective-permute-start(f32[1,2560]{1,0:T(1,128)S(1)} %constant_dynamic-update-slice_fusion.refs_1_), channel_id=1, source_target_pairs={{0,3},{1,2},{2,1},{3,0},{4,7},{5,6},{6,5},{7,4},{8,11},{9,10},{10,... | collective-permute-start | bytes 30728 | tf_op jit(solution)/shard_map/ppermute | solution.py:482
  157.6 1.9 %collective-permute-start.40 = (f32[1,2560]{1,0:T(1,128)S(1)}, f32[1,2560]{1,0:T(1,128)S(1)}, u32[]{:S(2)}, u32[]{:S(2)}) collective-permute-start(f32[1,2560]{1,0:T(1,128)S(1)} %constant_dynamic-update-slice_fusion.refs_1_), channel_id=1, source_target_pairs={{0,1},{1,0},{2,3},{3,2},{4,5},{5,4},{6,7},{7,6},{8,9},{9,8},{10,11... | collective-permute-start | bytes 30728 | tf_op jit(solution)/shard_map/ppermute | solution.py:482
  162.2 2.1 %shard_map.79 = (bf16[5120,256]{1,0:T(8,128)(2,1)}, bf16[10,256,256]{2,1,0:T(8,128)(2,1)S(1)}) custom-call(f32[256,2560]{1,0:T(8,128)S(1)} %get-tuple-element.28.refs_0_, f32[1,2560]{1,0:T(1,128)S(1)} %constant_dynamic-update-slice_fusion.refs_1_, f32[1,2560]{1,0:T(1,128)S(1)} %collective-permute-done.38.refs_2_, ...), custom_call_target="tpu_custom_call" | custom-call | flops 1310720 | bytes 7864320 | tf_op jit(solution)/shard_map/pallas_call | solution.py:332
  164.4 3.0 %collective-permute-done.41.half_ref = bf16[10,256,256]{2,1,0:T(8,128)(2,1)S(1)} collective-permute-done((bf16[10,256,256]{2,1,0:T(8,128)(2,1)S(1)}, bf16[10,256,256]{2,1,0:T(8,128)(2,1)S(1)}, u32[]{:S(2)}, u32[]{:S(2)}) %collective-permute-start.41) | collective-permute-done | bytes 1310752 | tf_op jit(solution)/shard_map/ppermute | solution.py:500
  (91 shorter events, 32.8 us)
Async XLA Ops:
  1.8 12.0 %collective-permute-start.13 = (bf16[128,1024]{1,0:T(8,128)(2,1)S(1)}, bf16[128,1024]{1,0:T(8,128)(2,1)S(1)}, u32[]{:S(2)}, u32[]{:S(2)}) collective-permute-start(bf16[128,1024]{1,0:T(8,128)(2,1)S(1)} %get-tuple-element.34), channel_id=1, source_target_pairs={{0,1},{3,2},{4,5},{7,6},{8,9},{11,10},{12,13},{15,14},{16,17},{19,... | collective-permute-start | bytes 786440 | tf_op jit(solution)/shard_map/ppermute | solution.py:380
  8.2 19.4 %collective-permute-start.5 = (bf16[128,1536]{1,0:T(8,128)(2,1)S(1)}, bf16[128,1536]{1,0:T(8,128)(2,1)S(1)}, u32[]{:S(2)}, u32[]{:S(2)}) collective-permute-start(bf16[128,1536]{1,0:T(8,128)(2,1)S(1)} %get-tuple-element.36), channel_id=1, source_target_pairs={{0,1},{3,2},{4,5},{7,6},{8,9},{11,10},{12,13},{15,14},{16,17},{19,... | collective-permute-start | bytes 1179656 | tf_op jit(solution)/shard_map/ppermute | solution.py:380
  9.7 17.8 %collective-permute-start.3 = (bf16[512,256]{1,0:T(8,128)(2,1)S(1)}, bf16[512,256]{1,0:T(8,128)(2,1)S(1)}, u32[]{:S(2)}, u32[]{:S(2)}) collective-permute-start(bf16[512,256]{1,0:T(8,128)(2,1)S(1)} %copy-done.2), channel_id=1, source_target_pairs={{0,1},{3,2},{4,5},{7,6},{8,9},{11,10},{12,13},{15,14},{16,17},{19,... | collective-permute-start | bytes 786440 | tf_op jit(solution)/shard_map/ppermute | solution.py:366
  12.5 27.9 %collective-permute-start = (bf16[128,1536]{1,0:T(8,128)(2,1)S(1)}, bf16[128,1536]{1,0:T(8,128)(2,1)S(1)}, u32[]{:S(2)}, u32[]{:S(2)}) collective-permute-start(bf16[128,1536]{1,0:T(8,128)(2,1)S(1)} %get-tuple-element.37), channel_id=1, source_target_pairs={{0,1},{3,2},{4,5},{7,6},{8,9},{11,10},{12,13},{15,14},{16,17},{19,... | collective-permute-start | bytes 1179656 | tf_op jit(solution)/shard_map/ppermute | solution.py:380
  13.9 27.1 %collective-permute-start.6 = (bf16[128,1536]{1,0:T(8,128)(2,1)S(1)}, bf16[128,1536]{1,0:T(8,128)(2,1)S(1)}, u32[]{:S(2)}, u32[]{:S(2)}) collective-permute-start(bf16[128,1536]{1,0:T(8,128)(2,1)S(1)} %get-tuple-element.36), channel_id=1, source_target_pairs={{0,4},{1,2},{2,1},{3,7},{4,0},{5,6},{6,5},{7,3},{8,12},{9,10},{10,... | collective-permute-start | bytes 1179656 | tf_op jit(solution)/shard_map/ppermute | solution.py:381
  13.9 26.5 %collective-permute-start.9 = (bf16[128,1024]{1,0:T(8,128)(2,1)S(1)}, bf16[128,1024]{1,0:T(8,128)(2,1)S(1)}, u32[]{:S(2)}, u32[]{:S(2)}) collective-permute-start(bf16[128,1024]{1,0:T(8,128)(2,1)S(1)} %get-tuple-element.35), channel_id=1, source_target_pairs={{0,1},{3,2},{4,5},{7,6},{8,9},{11,10},{12,13},{15,14},{16,17},{19,... | collective-permute-start | bytes 786440 | tf_op jit(solution)/shard_map/ppermute | solution.py:380
  27.5 13.5 %collective-permute-start.15 = (bf16[128,1024]{1,0:T(8,128)(2,1)S(1)}, bf16[128,1024]{1,0:T(8,128)(2,1)S(1)}, u32[]{:S(2)}, u32[]{:S(2)}) collective-permute-start(bf16[128,1024]{1,0:T(8,128)(2,1)S(1)} %collective-permute-done.13.refs_5_), channel_id=1, source_target_pairs={{0,4},{1,2},{2,1},{3,7},{4,0},{5,6},{6,5},{7,3},{8,12},{9,10},{10,... | collective-permute-start | bytes 786440 | tf_op jit(solution)/shard_map/ppermute | solution.py:382
  27.5 15.8 %collective-permute-start.7 = (bf16[128,1536]{1,0:T(8,128)(2,1)S(1)}, bf16[128,1536]{1,0:T(8,128)(2,1)S(1)}, u32[]{:S(2)}, u32[]{:S(2)}) collective-permute-start(bf16[128,1536]{1,0:T(8,128)(2,1)S(1)} %collective-permute-done.5.refs_5_), channel_id=1, source_target_pairs={{0,4},{1,2},{2,1},{3,7},{4,0},{5,6},{6,5},{7,3},{8,12},{9,10},{10,... | collective-permute-start | bytes 1179656 | tf_op jit(solution)/shard_map/ppermute | solution.py:382
  40.4 11.6 %collective-permute-start.1 = (bf16[128,1536]{1,0:T(8,128)(2,1)S(1)}, bf16[128,1536]{1,0:T(8,128)(2,1)S(1)}, u32[]{:S(2)}, u32[]{:S(2)}) collective-permute-start(bf16[128,1536]{1,0:T(8,128)(2,1)S(1)} %get-tuple-element.37), channel_id=1, source_target_pairs={{0,4},{1,2},{2,1},{3,7},{4,0},{5,6},{6,5},{7,3},{8,12},{9,10},{10,... | collective-permute-start | bytes 1179656 | tf_op jit(solution)/shard_map/ppermute | solution.py:381
  40.4 11.6 %collective-permute-start.2 = (bf16[128,1536]{1,0:T(8,128)(2,1)S(1)}, bf16[128,1536]{1,0:T(8,128)(2,1)S(1)}, u32[]{:S(2)}, u32[]{:S(2)}) collective-permute-start(bf16[128,1536]{1,0:T(8,128)(2,1)S(1)} %collective-permute-done.refs_5_), channel_id=1, source_target_pairs={{0,4},{1,2},{2,1},{3,7},{4,0},{5,6},{6,5},{7,3},{8,12},{9,10},{10,... | collective-permute-start | bytes 1179656 | tf_op jit(solution)/shard_map/ppermute | solution.py:382
  43.4 17.6 %collective-permute-start.16 = (s16[272,1024]{1,0:T(8,128)(2,1)S(1)}, s16[272,1024]{1,0:T(8,128)(2,1)S(1)}, u32[]{:S(2)}, u32[]{:S(2)}) collective-permute-start(s16[272,1024]{1,0:T(8,128)(2,1)S(1)} %shard_map.71), channel_id=1, source_target_pairs={{1,0},{2,3},{5,4},{6,7},{9,8},{10,11},{13,12},{14,15},{17,16},{18,... | collective-permute-start | bytes 1671176 | tf_op jit(solution)/shard_map/ppermute | solution.py:399
  47.4 68.4 %collective-permute-start.8 = (s16[272,1536]{1,0:T(8,128)(2,1)S(1)}, s16[272,1536]{1,0:T(8,128)(2,1)S(1)}, u32[]{:S(2)}, u32[]{:S(2)}) collective-permute-start(s16[272,1536]{1,0:T(8,128)(2,1)S(1)} %shard_map.69), channel_id=1, source_target_pairs={{1,0},{2,3},{5,4},{6,7},{9,8},{10,11},{13,12},{14,15},{17,16},{18,... | collective-permute-start | bytes 2506760 | tf_op jit(solution)/shard_map/ppermute | solution.py:399
  50.7 50.8 %collective-permute-start.12 = (s16[272,1024]{1,0:T(8,128)(2,1)S(1)}, s16[272,1024]{1,0:T(8,128)(2,1)S(1)}, u32[]{:S(2)}, u32[]{:S(2)}) collective-permute-start(s16[272,1024]{1,0:T(8,128)(2,1)S(1)} %shard_map.70), channel_id=1, source_target_pairs={{1,0},{2,3},{5,4},{6,7},{9,8},{10,11},{13,12},{14,15},{17,16},{18,... | collective-permute-start | bytes 1671176 | tf_op jit(solution)/shard_map/ppermute | solution.py:399
  54.7 68.1 %collective-permute-start.4 = (s16[272,1536]{1,0:T(8,128)(2,1)S(1)}, s16[272,1536]{1,0:T(8,128)(2,1)S(1)}, u32[]{:S(2)}, u32[]{:S(2)}) collective-permute-start(s16[272,1536]{1,0:T(8,128)(2,1)S(1)} %shard_map.68), channel_id=1, source_target_pairs={{1,0},{2,3},{5,4},{6,7},{9,8},{10,11},{13,12},{14,15},{17,16},{18,... | collective-permute-start | bytes 2506760 | tf_op jit(solution)/shard_map/ppermute | solution.py:399
  111.9 17.9 %collective-permute-start.31 = (f32[20,2048]{1,0:T(8,128)S(1)}, f32[20,2048]{1,0:T(8,128)S(1)}, u32[]{:S(2)}, u32[]{:S(2)}) collective-permute-start(f32[20,2048]{1,0:T(8,128)S(1)} %get-tuple-element.25.refs_1_), channel_id=1, source_target_pairs={{0,4},{4,0},{8,12},{12,8},{16,20},{20,16},{24,28},{28,24},{1,5},{5... | collective-permute-start | bytes 491528 | tf_op jit(solution)/shard_map/ppermute | solution.py:450
  114.6 16.5 %collective-permute-start.33 = (f32[20,2048]{1,0:T(8,128)S(1)}, f32[20,2048]{1,0:T(8,128)S(1)}, u32[]{:S(2)}, u32[]{:S(2)}) collective-permute-start(f32[20,2048]{1,0:T(8,128)S(1)} %collective-permute-done.32.refs_3_), channel_id=1, source_target_pairs={{0,4},{4,0},{8,12},{12,8},{16,20},{20,16},{24,28},{28,24},{1,5},{5... | collective-permute-start | bytes 491528 | tf_op jit(solution)/shard_map/ppermute | solution.py:450
  115.8 16.9 %collective-permute-start.35 = (f32[20,2048]{1,0:T(8,128)S(1)}, f32[20,2048]{1,0:T(8,128)S(1)}, u32[]{:S(2)}, u32[]{:S(2)}) collective-permute-start(f32[20,2048]{1,0:T(8,128)S(1)} %collective-permute-done.34.refs_5_), channel_id=1, source_target_pairs={{0,4},{4,0},{8,12},{12,8},{16,20},{20,16},{24,28},{28,24},{1,5},{5... | collective-permute-start | bytes 491528 | tf_op jit(solution)/shard_map/ppermute | solution.py:450
  115.9 16.9 %collective-permute-start.37 = (f32[20,2048]{1,0:T(8,128)S(1)}, f32[20,2048]{1,0:T(8,128)S(1)}, u32[]{:S(2)}, u32[]{:S(2)}) collective-permute-start(f32[20,2048]{1,0:T(8,128)S(1)} %collective-permute-done.36.refs_7_), channel_id=1, source_target_pairs={{0,4},{4,0},{8,12},{12,8},{16,20},{20,16},{24,28},{28,24},{1,5},{5... | collective-permute-start | bytes 491528 | tf_op jit(solution)/shard_map/ppermute | solution.py:450
  122.8 10.7 %collective-permute-start.25 = (f32[20,1536]{1,0:T(8,128)S(1)}, f32[20,1536]{1,0:T(8,128)S(1)}, u32[]{:S(2)}, u32[]{:S(2)}) collective-permute-start(f32[20,1536]{1,0:T(8,128)S(1)} %get-tuple-element.24.refs_1_), channel_id=1, source_target_pairs={{0,8},{4,12},{8,0},{12,4},{16,24},{20,28},{24,16},{28,20},{1,9},{5... | collective-permute-start | bytes 368648 | tf_op jit(solution)/shard_map/ppermute | solution.py:447
  129.9 9.5 %collective-permute-start.27 = (f32[20,1536]{1,0:T(8,128)S(1)}, f32[20,1536]{1,0:T(8,128)S(1)}, u32[]{:S(2)}, u32[]{:S(2)}) collective-permute-start(f32[20,1536]{1,0:T(8,128)S(1)} %get-tuple-element.24.refs_1_), channel_id=1, source_target_pairs={{0,16},{4,20},{8,24},{12,28},{16,0},{20,4},{24,8},{28,12},{1,17},{... | collective-permute-start | bytes 368648 | tf_op jit(solution)/shard_map/ppermute | solution.py:447
  131.1 10.8 %collective-permute-start.29 = (f32[20,1536]{1,0:T(8,128)S(1)}, f32[20,1536]{1,0:T(8,128)S(1)}, u32[]{:S(2)}, u32[]{:S(2)}) collective-permute-start(f32[20,1536]{1,0:T(8,128)S(1)} %get-tuple-element.24.refs_1_), channel_id=1, source_target_pairs={{0,24},{4,28},{8,16},{12,20},{16,8},{20,12},{24,0},{28,4},{1,25},{... | collective-permute-start | bytes 368648 | tf_op jit(solution)/shard_map/ppermute | solution.py:447
  132.8 9.1 %collective-permute-start.24 = (f32[20,1536]{1,0:T(8,128)S(1)}, f32[20,1536]{1,0:T(8,128)S(1)}, u32[]{:S(2)}, u32[]{:S(2)}) collective-permute-start(f32[20,1536]{1,0:T(8,128)S(1)} %get-tuple-element.24.refs_1_), channel_id=1, source_target_pairs={{0,4},{4,0},{8,12},{12,8},{16,20},{20,16},{24,28},{28,24},{1,5},{5... | collective-permute-start | bytes 368648 | tf_op jit(solution)/shard_map/ppermute | solution.py:450
  132.8 9.6 %collective-permute-start.18 = (f32[20,1536]{1,0:T(8,128)S(1)}, f32[20,1536]{1,0:T(8,128)S(1)}, u32[]{:S(2)}, u32[]{:S(2)}) collective-permute-start(f32[20,1536]{1,0:T(8,128)S(1)} %get-tuple-element.23.refs_1_), channel_id=1, source_target_pairs={{0,8},{4,12},{8,0},{12,4},{16,24},{20,28},{24,16},{28,20},{1,9},{5... | collective-permute-start | bytes 368648 | tf_op jit(solution)/shard_map/ppermute | solution.py:447
  133.5 13.3 %collective-permute-start.20 = (f32[20,1536]{1,0:T(8,128)S(1)}, f32[20,1536]{1,0:T(8,128)S(1)}, u32[]{:S(2)}, u32[]{:S(2)}) collective-permute-start(f32[20,1536]{1,0:T(8,128)S(1)} %get-tuple-element.23.refs_1_), channel_id=1, source_target_pairs={{0,16},{4,20},{8,24},{12,28},{16,0},{20,4},{24,8},{28,12},{1,17},{... | collective-permute-start | bytes 368648 | tf_op jit(solution)/shard_map/ppermute | solution.py:447
  (24 other events, 246.3 us)
